TPU v7x, 256 devices: a whole 4x4x8 slice. The times are simulated.
256 devices in a mesh: dp: 4 (over y), ep: 64 (over z, x, core).
Axes of the slice: x: 4, y: 4, z: 8, core: 2. Of those that a mesh axis runs over, the one named last changes fastest.
Arguments:
- tokens: bfloat16 [32768, 7168], P(('dp', 'ep')), may hold values from -6 to 6
- out_grad: bfloat16 [32768, 7168], P(('dp', 'ep')), may hold values from -3 to 3
- route_weight: float32 [32768, 1], P(('dp', 'ep')), may hold values from 0.2 to 1
- expert_ids: int32 [32768, 1], P(('dp', 'ep')), may hold values from 0 to 15
- w_gate: bfloat16 [1024, 114688], P('dp', 'ep'), may hold values from -0.0625 to 0.0625
- w_up: bfloat16 [1024, 114688], P('dp', 'ep'), may hold values from -0.0625 to 0.0625
- w_down: bfloat16 [1024, 114688], P('dp', 'ep'), may hold values from -0.1875 to 0.1875
Outputs:
- in_grad: bfloat16 [32768, 7168], P(('dp', 'ep'))
- grad_gate: bfloat16 [1024, 114688], P('dp', 'ep')
- grad_up: bfloat16 [1024, 114688], P('dp', 'ep')
- grad_down: bfloat16 [1024, 114688], P('dp', 'ep')
All inputs are finite; a program needn't handle non-finite values.
Results may differ from a plain program's by a relative error of at most 0.012.
Values may be sent and summed in bfloat16 or wider, within the bound.
A program may use at most 128 MiB of HBM per device.

v0:
```python
import jax
import jax.numpy as jnp
from jax import lax
from jax.sharding import PartitionSpec as P

D = 7168
GROUP = 4
TOP = 1


CONTRACT_LAST = (((1,), (1,)), ((), ()))
CONTRACT_FIRST = (((0,), (0,)), ((), ()))


def in_one_piece(arrays, axis, dim, along):
    ends, at = ([], 0)
    for a in arrays[:-1]:
        at += a.shape[along]
        ends.append(at)
    both = jnp.concatenate(arrays, axis=along)
    return tuple(jnp.split(lax.all_gather(both, axis, axis=dim, tiled=True), ends, axis=along))


def as_sent(value):

    def short(part):
        return part.astype(jnp.bfloat16) if part.dtype == jnp.float32 else part

    return jax.tree.map(short, value)


def from_partner(value, axis, distance):
    mask = 2**distance
    pairs = [(source, source ^ mask) for source in range(lax.axis_size(axis))]
    return lax.ppermute(value, axis, pairs)


def slot_tables(expert_ids, route_weight, experts, capacity):
    token_count, top_count = expert_ids.shape
    pair_count = token_count * top_count
    flat_ids = expert_ids.reshape(pair_count)
    onehot = (flat_ids[:, None] == jnp.arange(experts, dtype=jnp.int32)[None, :]).astype(jnp.int32)
    before = jnp.cumsum(onehot, axis=0) - onehot
    ranks = jnp.sum(before * onehot, axis=1)
    kept = ranks < capacity
    slots = jnp.where(kept, flat_ids * capacity + ranks, 0)
    slot_ids = jnp.arange(experts * capacity, dtype=jnp.int32)
    match = (slots[None, :] == slot_ids[:, None]) & kept[None, :]
    pair_ids = jnp.arange(pair_count, dtype=jnp.int32)
    pair_of_slot = jnp.sum(jnp.where(match, pair_ids[None, :], 0), axis=1)
    filled = jnp.any(match, axis=1)
    flat_weight = route_weight.reshape(pair_count)
    weight_of_slot = jnp.sum(jnp.where(match, flat_weight[None, :], jnp.float32(0.0)), axis=1)
    return (kept, slots, pair_of_slot // top_count, filled, weight_of_slot)


def activations(gate, up, back):
    logistic = jax.nn.sigmoid(gate)
    silu = gate * logistic
    hidden = (silu * up).astype(jnp.bfloat16)
    d_gate = (back * up * logistic * (1.0 + gate * (1.0 - logistic))).astype(jnp.bfloat16)
    d_up = (back * silu).astype(jnp.bfloat16)
    return (hidden, d_gate, d_up)


def to_owners(rows, experts, capacity, quarter):
    shaped = rows.reshape(experts, capacity, GROUP, quarter).transpose(0, 2, 1, 3)
    return shaped.reshape(experts * GROUP, capacity, quarter)


def body(tokens, out_grad, route_weight, expert_ids, w_gate, w_up, w_down):
    devices_ep = lax.axis_size("ep")
    experts = devices_ep // GROUP
    token_count = tokens.shape[0]
    capacity = 6 * GROUP * token_count * TOP // (8 * devices_ep)
    quarter = D // GROUP
    levels = GROUP.bit_length() - 1
    kept, slots, token_of_slot, filled, weight_of_slot = slot_tables(
        expert_ids, route_weight, experts, capacity
    )
    x_slots = jnp.take(tokens, token_of_slot, axis=0) * filled[:, None].astype(jnp.bfloat16)
    d_slots = (
        jnp.take(out_grad, token_of_slot, axis=0).astype(jnp.float32) * weight_of_slot[:, None]
    ).astype(jnp.bfloat16)
    x_send = to_owners(x_slots, experts, capacity, quarter)
    d_send = to_owners(d_slots, experts, capacity, quarter)
    x_recv, d_recv = (
        lax.all_to_all(x_send, "ep", split_axis=0, concat_axis=0, tiled=True),
        lax.all_to_all(d_send, "ep", split_axis=0, concat_axis=0, tiled=True),
    )
    row_count = x_recv.shape[0] * x_recv.shape[1]
    x_rows = x_recv.reshape(row_count, quarter)
    d_rows = d_recv.reshape(row_count, quarter)
    gate_w, up_w, down_w = in_one_piece((w_gate, w_up, w_down), "dp", 0, 1)
    x_used, d_used = (x_rows, d_rows)
    gate_part = lax.dot_general(
        x_used, gate_w, CONTRACT_LAST, preferred_element_type=jnp.float32
    ).astype(jnp.bfloat16)
    up_part = lax.dot_general(
        x_used, up_w, CONTRACT_LAST, preferred_element_type=jnp.float32
    ).astype(jnp.bfloat16)
    back_part = lax.dot_general(
        d_used, down_w, CONTRACT_LAST, preferred_element_type=jnp.float32
    ).astype(jnp.bfloat16)
    member = lax.axis_index("ep") % GROUP
    pieces = (gate_part[None], up_part[None], back_part[None])
    width = gate_part.shape[1]
    for bit in reversed(range(levels)):
        half = width // 2
        side = member // (1 << bit) % 2
        keep = tuple((lax.dynamic_slice_in_dim(piece, side * half, half, 2) for piece in pieces))
        give = tuple(
            (lax.dynamic_slice_in_dim(piece, (1 - side) * half, half, 2) for piece in pieces)
        )
        received = jax.tree.map(
            lambda part, own: part.astype(own.dtype), from_partner(as_sent(give), "ep", bit), give
        )
        pieces = tuple(
            (jnp.concatenate([mine, theirs], axis=0) for mine, theirs in zip(keep, received))
        )
        width = half
    gate = jnp.sum(pieces[0].astype(jnp.float32), axis=0)
    up = jnp.sum(pieces[1].astype(jnp.float32), axis=0)
    back = jnp.sum(pieces[2].astype(jnp.float32), axis=0)
    shares = activations(gate, up, back)
    for bit in range(levels):
        side = member // (1 << bit) % 2
        other = jax.tree.map(
            lambda part, own: part.astype(own.dtype),
            from_partner(as_sent(shares), "ep", bit),
            shares,
        )
        shares = tuple(
            (
                jnp.where(
                    side == 0,
                    jnp.concatenate([mine, theirs], axis=1),
                    jnp.concatenate([theirs, mine], axis=1),
                )
                for mine, theirs in zip(shares, other)
            )
        )
    hidden, d_gate, d_up = shares
    expert_dx = (
        jnp.dot(d_gate, gate_w, preferred_element_type=jnp.float32)
        + jnp.dot(d_up, up_w, preferred_element_type=jnp.float32)
    ).astype(jnp.bfloat16)
    gate_term = lax.dot_general(d_gate, x_rows, CONTRACT_FIRST, preferred_element_type=jnp.float32)
    up_term = lax.dot_general(d_up, x_rows, CONTRACT_FIRST, preferred_element_type=jnp.float32)
    down_term = lax.dot_general(hidden, d_rows, CONTRACT_FIRST, preferred_element_type=jnp.float32)
    sums = lax.psum_scatter(
        jnp.concatenate([gate_term, up_term, down_term], axis=1).astype(jnp.bfloat16),
        "dp",
        scatter_dimension=0,
        tiled=True,
    ).astype(jnp.float32)
    grad_gate = sums[:, :quarter].astype(jnp.bfloat16)
    grad_up = sums[:, quarter : 2 * quarter].astype(jnp.bfloat16)
    grad_down = sums[:, 2 * quarter :].astype(jnp.bfloat16)
    returned = lax.all_to_all(
        expert_dx.reshape(devices_ep, capacity, quarter),
        "ep",
        split_axis=0,
        concat_axis=0,
        tiled=True,
    )
    slot_rows = (
        returned.reshape(experts, GROUP, capacity, quarter)
        .transpose(0, 2, 1, 3)
        .reshape(experts * capacity, D)
    )
    pair_rows = jnp.take(slot_rows, slots, axis=0) * kept[:, None].astype(jnp.bfloat16)
    in_grad = jnp.sum(pair_rows.reshape(token_count, TOP, D).astype(jnp.float32), axis=1).astype(
        jnp.bfloat16
    )
    return (in_grad, grad_gate, grad_up, grad_down)


def solution(mesh):
    placed = (
        P(("dp", "ep"), None),
        P(("dp", "ep"), None),
        P(("dp", "ep"), None),
        P(("dp", "ep"), None),
        P("dp", "ep"),
        P("dp", "ep"),
        P("dp", "ep"),
    )
    return jax.shard_map(
        body,
        mesh=mesh,
        in_specs=placed,
        out_specs=(P(("dp", "ep"), None), P("dp", "ep"), P("dp", "ep"), P("dp", "ep")),
        check_vma=False,
    )
```

profile of v0, /device:TPU:1, one launch (start us, length us, event | category | flops | bytes accessed | tf_op | source)
XLA Modules:
  0.0 314.9 jit_solution(9663100662735243545)
XLA Ops:
  7.2 3.7 %pad_maximum_fusion.1 = bf16[256,5376]{1,0:T(8,128)(2,1)} fusion(bf16[256,1792]{1,0:T(8,128)(2,1)} %param.15, bf16[256,1792]{1,0:T(8,128)(2,1)} %param.14, bf16[256,1792]{1,0:T(8,128)(2,1)} %param.13), kind=kLoop, calls=%fused_computation.19 | loop fusion | flops 8257536 | bytes 5505024 | tf_op jit(solution)/shard_map/concatenate | solution.py:20
  10.9 0.6 copy-done.10
  12.3 1.4 gather_fusion.2
  13.7 0.2 select_multiply_fusion.1
  13.9 1.1 reshape.100
  15.0 1.5 copy.28
  16.5 13.3 %all-to-all-start.1 = ((bf16[64,6,1792]{2,1,0:T(8,128)(2,1)}), bf16[64,6,1792]{2,1,0:T(8,128)(2,1)}, u32[]{:S(2)}, u32[]{:S(2)}) async-start(bf16[64,6,1792]{2,1,0:T(8,128)(2,1)} %bitcast.42), calls=%async_computation.1 | async-start | bytes 3670016 | tf_op jit(solution)/shard_map/all_to_all | solution.py:88
  29.8 1.4 gather_fusion.1
  31.3 0.4 multiply_convert_fusion
  31.7 1.1 reshape.97
  32.8 1.5 copy.27
  34.3 39.8 %all-to-all-done.1 = bf16[64,6,1792]{2,1,0:T(8,128)(2,1)} async-done(((bf16[64,6,1792]{2,1,0:T(8,128)(2,1)}), bf16[64,6,1792]{2,1,0:T(8,128)(2,1)}, u32[]{:S(2)}, u32[]{:S(2)}) %all-to-all-start.1) | async-done | bytes 1376288 | tf_op jit(solution)/shard_map/all_to_all | solution.py:88
  74.1 6.6 %all-to-all-start = ((bf16[64,6,1792]{2,1,0:T(8,128)(2,1)}), bf16[64,6,1792]{2,1,0:T(8,128)(2,1)S(1)}, u32[]{:S(2)}, u32[]{:S(2)}) async-start(bf16[64,6,1792]{2,1,0:T(8,128)(2,1)} %bitcast.5), calls=%async_computation | async-start | bytes 3670016 | tf_op jit(solution)/shard_map/all_to_all | solution.py:89
  80.9 2.5 reshape.102
  83.3 41.8 %all-to-all-done = bf16[64,6,1792]{2,1,0:T(8,128)(2,1)S(1)} async-done(((bf16[64,6,1792]{2,1,0:T(8,128)(2,1)}), bf16[64,6,1792]{2,1,0:T(8,128)(2,1)S(1)}, u32[]{:S(2)}, u32[]{:S(2)}) %all-to-all-start) | async-done | bytes 1376288 | tf_op jit(solution)/shard_map/all_to_all | solution.py:89
  125.2 1.3 reshape.99
  126.5 3.8 %fusion.19 = bf16[384,1024]{1,0:T(8,128)(2,1)S(1)} fusion(bf16[384,1792]{1,0:T(8,128)(2,1)S(1)} %reshape.102, bf16[1024,5376]{1,0:T(8,128)(2,1)} %all-gather.2.cloned.1.call-done), kind=kOutput, calls=%fused_computation.26 | convolution fusion | flops 1409679360 | bytes 5832704 | tf_op jit(solution)/shard_map/dot_general | solution.py:96
  130.3 0.8 dynamic-slice_bitcast_fusion
  131.1 0.9 collective-permute-start.4
  132.0 1.6 fusion.16
  133.7 0.8 dynamic-slice_bitcast_fusion.2
  134.5 0.7 collective-permute-start.2
  135.2 1.6 fusion.22
  136.8 0.8 dynamic-slice_bitcast_fusion.4
  137.7 0.7 collective-permute-start
  138.4 1.9 collective-permute-done.4
  140.3 0.7 copy-done.5
  141.0 1.1 fusion.32
  142.1 4.9 %collective-permute-start.5 = (bf16[2,384,256]{2,1,0:T(8,128)(2,1)S(1)}, bf16[2,384,256]{2,1,0:T(8,128)(2,1)S(1)}, u32[]{:S(2)}, u32[]{:S(2)}) collective-permute-start(bf16[2,384,256]{2,1,0:T(8,128)(2,1)S(1)} %get-tuple-element.18), channel_id=1, source_target_pairs={{0,1},{1,0},{2,3},{3,2},{4,5},{5,4},{6,7},{7,6},{8,9},{9,8},{10,11... | collective-permute-start | bytes 1179656 | tf_op jit(solution)/shard_map/ppermute | solution.py:35
  147.0 1.8 collective-permute-done.2
  148.8 1.1 fusion.34
  149.9 4.9 %collective-permute-start.3 = (bf16[2,384,256]{2,1,0:T(8,128)(2,1)S(1)}, bf16[2,384,256]{2,1,0:T(8,128)(2,1)S(1)}, u32[]{:S(2)}, u32[]{:S(2)}) collective-permute-start(bf16[2,384,256]{2,1,0:T(8,128)(2,1)S(1)} %get-tuple-element.14), channel_id=1, source_target_pairs={{0,1},{1,0},{2,3},{3,2},{4,5},{5,4},{6,7},{7,6},{8,9},{9,8},{10,11... | collective-permute-start | bytes 1179656 | tf_op jit(solution)/shard_map/ppermute | solution.py:35
  154.8 2.4 collective-permute-done
  157.2 1.1 fusion.36
  158.3 2.7 collective-permute-start.1
  161.2 1.1 collective-permute-done.1
  162.4 0.3 multiply_convert_fusion.1
  162.7 0.5 collective-permute-start.10
  163.3 1.1 collective-permute-done.10
  164.4 1.9 maximum_select_fusion.6
  166.3 0.9 collective-permute-start.11
  167.2 0.7 collective-permute-start.8
  167.8 1.1 maximum_select_fusion.4
  168.9 0.7 collective-permute-start.7
  169.7 1.0 collective-permute-start.9
  170.7 6.2 %collective-permute-done.11 = bf16[384,512]{1,0:T(8,128)(2,1)} collective-permute-done((bf16[384,512]{1,0:T(8,128)(2,1)}, bf16[384,512]{1,0:T(8,128)(2,1)}, u32[]{:S(2)}, u32[]{:S(2)}) %collective-permute-start.11) | collective-permute-done | bytes 393248 | tf_op jit(solution)/shard_map/ppermute | solution.py:35
  176.9 3.5 %convolution_convert_fusion = bf16[1024,1792]{1,0:T(8,128)(2,1)S(1)} fusion(bf16[384,1792]{1,0:T(8,128)(2,1)S(1)} %copy-done.4, bf16[384,512]{1,0:T(8,128)(2,1)} %collective-permute-done.11, bf16[384,512]{1,0:T(8,128)(2,1)} %maximum_select_fusion.6, pred[]{:T(512)S(6)} %eq.48), kind=kOutput, calls=%fused_computation.4 | convolution fusion | flops 1414660096 | bytes 5832705 | tf_op jit(solution)/shard_map/dot_general | solution.py:150
  180.4 4.8 %collective-permute-done.7 = bf16[384,512]{1,0:T(8,128)(2,1)S(1)} collective-permute-done((bf16[384,512]{1,0:T(8,128)(2,1)S(1)}, bf16[384,512]{1,0:T(8,128)(2,1)S(1)}, u32[]{:S(2)}, u32[]{:S(2)}) %collective-permute-start.7) | collective-permute-done | bytes 393248 | tf_op jit(solution)/shard_map/ppermute | solution.py:35
  185.2 2.1 convolution_convert_fusion.2
  187.3 6.3 %collective-permute-done.9 = bf16[384,512]{1,0:T(8,128)(2,1)S(1)} collective-permute-done((bf16[384,512]{1,0:T(8,128)(2,1)S(1)}, bf16[384,512]{1,0:T(8,128)(2,1)S(1)}, u32[]{:S(2)}, u32[]{:S(2)}) %collective-permute-start.9) | collective-permute-done | bytes 393248 | tf_op jit(solution)/shard_map/ppermute | solution.py:35
  193.6 0.7 copy-done.15
  194.4 2.1 convolution_convert_fusion.1
  196.5 5.7 %pad_maximum_fusion = bf16[1024,5376]{1,0:T(8,128)(2,1)} fusion(bf16[1024,1792]{1,0:T(8,128)(2,1)S(1)} %convolution_convert_fusion, bf16[1024,1792]{1,0:T(8,128)(2,1)S(1)} %convolution_convert_fusion.1, bf16[1024,1792]{1,0:T(8,128)(2,1)S(1)} %convolution_convert_fusion.2), kind=kLoop, calls=%fused_computation.3 | loop fusion | flops 33030144 | bytes 22020096 | tf_op jit(solution)/shard_map/concatenate | solution.py:152
  202.2 1.0 copy-done.9
  203.3 3.7 %fusion.6 = f32[384,1792]{1,0:T(8,128)S(1)} fusion(bf16[1024,5376]{1,0:T(8,128)(2,1)} %all-gather.2.cloned.1.call-done, bf16[384,512]{1,0:T(8,128)(2,1)S(1)} %copy-done.16, bf16[384,512]{1,0:T(8,128)(2,1)S(1)} %copy-done.9, pred[]{:T(512)S(6)} %eq.48), kind=kOutput, calls=%fused_computation.13 | convolution fusion | flops 1412825088 | bytes 7208961 | tf_op jit(solution)/shard_map/dot_general | solution.py:146
  207.1 3.6 %fusion.13 = bf16[384,1792]{1,0:T(8,128)(2,1)S(1)} fusion(f32[384,1792]{1,0:T(8,128)S(1)} %fusion.6, bf16[1024,5376]{1,0:T(8,128)(2,1)} %all-gather.2.cloned.1.call-done, bf16[384,512]{1,0:T(8,128)(2,1)S(1)} %copy-done.14, bf16[384,512]{1,0:T(8,128)(2,1)S(1)} %copy-done.7, pred[]{:T(512)S(6)} %eq.48), kind=kOutput, calls=%fused_computation.18 | convolution fusion | flops 1414201344 | bytes 8585217 | tf_op jit(solution)/shard_map/dot_general | solution.py:145
  210.7 1.5 reshape.103
  212.2 7.3 %all-to-all-start.2 = ((bf16[64,6,1792]{2,1,0:T(8,128)(2,1)}), bf16[64,6,1792]{2,1,0:T(8,128)(2,1)S(1)}, u32[]{:S(2)}, u32[]{:S(2)}) async-start(bf16[64,6,1792]{2,1,0:T(8,128)(2,1)} %reshape.103), calls=%async_computation.2 | async-start | bytes 3670016 | tf_op jit(solution)/shard_map/all_to_all | solution.py:160
  219.5 44.4 %all-to-all-done.2 = bf16[64,6,1792]{2,1,0:T(8,128)(2,1)S(1)} async-done(((bf16[64,6,1792]{2,1,0:T(8,128)(2,1)}), bf16[64,6,1792]{2,1,0:T(8,128)(2,1)S(1)}, u32[]{:S(2)}, u32[]{:S(2)}) %all-to-all-start.2) | async-done | bytes 1376288 | tf_op jit(solution)/shard_map/all_to_all | solution.py:160
  263.9 0.5 copy.26
  264.6 2.9 gather_fusion
  267.5 3.1 select_multiply_fusion
  270.6 34.1 %reduce-scatter.2.cloned.1.call-done = bf16[256,5376]{1,0:T(8,128)(2,1)} async-done(((bf16[1024,5376]{1,0:T(8,128)(2,1)}), bf16[256,5376]{1,0:T(8,128)(2,1)}) %reduce-scatter.2.cloned.1.call-update) | async-done | bytes 2752528 | tf_op jit(solution)/shard_map/reduce_scatter | solution.py:151
  304.8 3.3 %fusion.47 = (bf16[256,1792]{1,0:T(8,128)(2,1)}, bf16[256,1792]{1,0:T(8,128)(2,1)}, bf16[256,1792]{1,0:T(8,128)(2,1)}) fusion(bf16[256,5376]{1,0:T(8,128)(2,1)} %reduce-scatter.2.cloned.1.call-done), kind=kLoop, calls=%fused_computation.94 | loop fusion | bytes 5505024 | tf_op jit(solution)/shard_map/slice | solution.py:159
  (59 shorter events, 1.8 us)
Async XLA Ops:
  7.2 5.1 %copy-start = (bf16[128,7168]{1,0:T(8,128)(2,1)S(1)}, bf16[128,7168]{1,0:T(8,128)(2,1)}, u32[]{:S(2)}) copy-start(bf16[128,7168]{1,0:T(8,128)(2,1)} %param.9) | copy-start | bytes 5505028
  7.2 119.3 %all-gather.2.cloned.1.call-start = ((), (), s32[]{:S(2)}) async-start(), calls=%async_computation.4 | async-start | bytes 13762560 | tf_op jit(solution)/shard_map/all_gather | solution.py:21
  10.9 0.7 copy-start.10
  16.5 13.3 %copy-start.2 = (bf16[128,7168]{1,0:T(8,128)(2,1)S(1)}, bf16[128,7168]{1,0:T(8,128)(2,1)}, u32[]{:S(2)}) copy-start(bf16[128,7168]{1,0:T(8,128)(2,1)} %param.10) | copy-start | bytes 5505028
  16.5 57.6 %all-to-all-start.1 = ((bf16[64,6,1792]{2,1,0:T(8,128)(2,1)}), bf16[64,6,1792]{2,1,0:T(8,128)(2,1)}, u32[]{:S(2)}, u32[]{:S(2)}) async-start(bf16[64,6,1792]{2,1,0:T(8,128)(2,1)} %bitcast.42), calls=%async_computation.1 | async-start | bytes 3670016 | tf_op jit(solution)/shard_map/all_to_all | solution.py:88
  29.8 1.4 copy-start.11
  74.1 51.1 %all-to-all-start = ((bf16[64,6,1792]{2,1,0:T(8,128)(2,1)}), bf16[64,6,1792]{2,1,0:T(8,128)(2,1)S(1)}, u32[]{:S(2)}, u32[]{:S(2)}) async-start(bf16[64,6,1792]{2,1,0:T(8,128)(2,1)} %bitcast.5), calls=%async_computation | async-start | bytes 3670016 | tf_op jit(solution)/shard_map/all_to_all | solution.py:89
  80.8 224.0 %reduce-scatter.2.cloned.1.call-start = ((), (), s32[]{:S(2)}) async-start(), calls=%async_computation.5 | async-start | bytes 13762560 | tf_op jit(solution)/shard_map/reduce_scatter | solution.py:151
  126.5 5.5 %copy-start.12 = (bf16[1024,5376]{1,0:T(8,128)(2,1)S(1)}, bf16[1024,5376]{1,0:T(8,128)(2,1)}, u32[]{:S(2)}) copy-start(bf16[1024,5376]{1,0:T(8,128)(2,1)} %all-gather.2.cloned.1.call-done) | copy-start | bytes 33030148
  131.1 4.1 %copy-start.3 = (bf16[384,1792]{1,0:T(8,128)(2,1)S(1)}, bf16[384,1792]{1,0:T(8,128)(2,1)}, u32[]{:S(2)}) copy-start(bf16[384,1792]{1,0:T(8,128)(2,1)} %reshape.99) | copy-start | bytes 4128772
  131.1 9.1 %collective-permute-start.4 = (bf16[1,384,512]{2,1,0:T(8,128)(2,1)}, bf16[1,384,512]{2,1,0:T(8,128)(2,1)S(1)}, u32[]{:S(2)}, u32[]{:S(2)}) collective-permute-start(bf16[1,384,512]{2,1,0:T(8,128)(2,1)} %get-tuple-element.19), channel_id=1, source_target_pairs={{0,2},{1,3},{2,0},{3,1},{4,6},{5,7},{6,4},{7,5},{8,10},{9,11},{10,... | collective-permute-start | bytes 1179656 | tf_op jit(solution)/shard_map/ppermute | solution.py:35
  134.5 14.3 %collective-permute-start.2 = (bf16[1,384,512]{2,1,0:T(8,128)(2,1)}, bf16[1,384,512]{2,1,0:T(8,128)(2,1)}, u32[]{:S(2)}, u32[]{:S(2)}) collective-permute-start(bf16[1,384,512]{2,1,0:T(8,128)(2,1)} %get-tuple-element.15), channel_id=1, source_target_pairs={{0,2},{1,3},{2,0},{3,1},{4,6},{5,7},{6,4},{7,5},{8,10},{9,11},{10,... | collective-permute-start | bytes 1179656 | tf_op jit(solution)/shard_map/ppermute | solution.py:35
  137.7 19.5 %collective-permute-start = (bf16[1,384,512]{2,1,0:T(8,128)(2,1)}, bf16[1,384,512]{2,1,0:T(8,128)(2,1)}, u32[]{:S(2)}, u32[]{:S(2)}) collective-permute-start(bf16[1,384,512]{2,1,0:T(8,128)(2,1)} %get-tuple-element.23), channel_id=1, source_target_pairs={{0,2},{1,3},{2,0},{3,1},{4,6},{5,7},{6,4},{7,5},{8,10},{9,11},{10,... | collective-permute-start | bytes 1179656 | tf_op jit(solution)/shard_map/ppermute | solution.py:35
  140.3 0.7 copy-start.5
  142.1 18.9 %collective-permute-start.5 = (bf16[2,384,256]{2,1,0:T(8,128)(2,1)S(1)}, bf16[2,384,256]{2,1,0:T(8,128)(2,1)S(1)}, u32[]{:S(2)}, u32[]{:S(2)}) collective-permute-start(bf16[2,384,256]{2,1,0:T(8,128)(2,1)S(1)} %get-tuple-element.18), channel_id=1, source_target_pairs={{0,1},{1,0},{2,3},{3,2},{4,5},{5,4},{6,7},{7,6},{8,9},{9,8},{10,11... | collective-permute-start | bytes 1179656 | tf_op jit(solution)/shard_map/ppermute | solution.py:35
  149.9 11.2 %collective-permute-start.3 = (bf16[2,384,256]{2,1,0:T(8,128)(2,1)S(1)}, bf16[2,384,256]{2,1,0:T(8,128)(2,1)S(1)}, u32[]{:S(2)}, u32[]{:S(2)}) collective-permute-start(bf16[2,384,256]{2,1,0:T(8,128)(2,1)S(1)} %get-tuple-element.14), channel_id=1, source_target_pairs={{0,1},{1,0},{2,3},{3,2},{4,5},{5,4},{6,7},{7,6},{8,9},{9,8},{10,11... | collective-permute-start | bytes 1179656 | tf_op jit(solution)/shard_map/ppermute | solution.py:35
  158.3 4.0 %collective-permute-start.1 = (bf16[2,384,256]{2,1,0:T(8,128)(2,1)S(1)}, bf16[2,384,256]{2,1,0:T(8,128)(2,1)S(1)}, u32[]{:S(2)}, u32[]{:S(2)}) collective-permute-start(bf16[2,384,256]{2,1,0:T(8,128)(2,1)S(1)} %get-tuple-element.22), channel_id=1, source_target_pairs={{0,1},{1,0},{2,3},{3,2},{4,5},{5,4},{6,7},{7,6},{8,9},{9,8},{10,11... | collective-permute-start | bytes 1179656 | tf_op jit(solution)/shard_map/ppermute | solution.py:35
  162.7 14.2 %copy-start.4 = (bf16[384,1792]{1,0:T(8,128)(2,1)S(1)}, bf16[384,1792]{1,0:T(8,128)(2,1)}, u32[]{:S(2)}) copy-start(bf16[384,1792]{1,0:T(8,128)(2,1)} %reshape.99) | copy-start | bytes 4128772
  162.7 1.7 collective-permute-start.10
  163.2 4.6 %collective-permute-start.6 = (bf16[384,256]{1,0:T(8,128)(2,1)S(1)}, bf16[384,256]{1,0:T(8,128)(2,1)}, u32[]{:S(2)}, u32[]{:S(2)}) collective-permute-start(bf16[384,256]{1,0:T(8,128)(2,1)S(1)} %get-tuple-element.11), channel_id=1, source_target_pairs={{0,1},{1,0},{2,3},{3,2},{4,5},{5,4},{6,7},{7,6},{8,9},{9,8},{10,11... | collective-permute-start | bytes 589832 | tf_op jit(solution)/shard_map/ppermute | solution.py:35
  166.3 10.6 %collective-permute-start.11 = (bf16[384,512]{1,0:T(8,128)(2,1)}, bf16[384,512]{1,0:T(8,128)(2,1)}, u32[]{:S(2)}, u32[]{:S(2)}) collective-permute-start(bf16[384,512]{1,0:T(8,128)(2,1)} %maximum_select_fusion.6), channel_id=1, source_target_pairs={{0,2},{1,3},{2,0},{3,1},{4,6},{5,7},{6,4},{7,5},{8,10},{9,11},{10,... | collective-permute-start | bytes 1179656 | tf_op jit(solution)/shard_map/ppermute | solution.py:35
  167.2 2.4 collective-permute-start.8
  168.9 16.3 %copy-start.6 = (bf16[384,512]{1,0:T(8,128)(2,1)}, bf16[384,512]{1,0:T(8,128)(2,1)S(1)}, u32[]{:S(2)}) copy-start(bf16[384,512]{1,0:T(8,128)(2,1)S(1)} %maximum_select_fusion.4) | copy-start | bytes 1179652
  168.9 16.3 %collective-permute-start.7 = (bf16[384,512]{1,0:T(8,128)(2,1)S(1)}, bf16[384,512]{1,0:T(8,128)(2,1)S(1)}, u32[]{:S(2)}, u32[]{:S(2)}) collective-permute-start(bf16[384,512]{1,0:T(8,128)(2,1)S(1)} %maximum_select_fusion.4), channel_id=1, source_target_pairs={{0,2},{1,3},{2,0},{3,1},{4,6},{5,7},{6,4},{7,5},{8,10},{9,11},{10,... | collective-permute-start | bytes 1179656 | tf_op jit(solution)/shard_map/ppermute | solution.py:35
  169.7 23.9 %copy-start.8 = (bf16[384,512]{1,0:T(8,128)(2,1)}, bf16[384,512]{1,0:T(8,128)(2,1)S(1)}, u32[]{:S(2)}) copy-start(bf16[384,512]{1,0:T(8,128)(2,1)S(1)} %maximum_select_fusion.5) | copy-start | bytes 1179652
  169.7 23.9 %collective-permute-start.9 = (bf16[384,512]{1,0:T(8,128)(2,1)S(1)}, bf16[384,512]{1,0:T(8,128)(2,1)S(1)}, u32[]{:S(2)}, u32[]{:S(2)}) collective-permute-start(bf16[384,512]{1,0:T(8,128)(2,1)S(1)} %maximum_select_fusion.5), channel_id=1, source_target_pairs={{0,2},{1,3},{2,0},{3,1},{4,6},{5,7},{6,4},{7,5},{8,10},{9,11},{10,... | collective-permute-start | bytes 1179656 | tf_op jit(solution)/shard_map/ppermute | solution.py:35
  185.2 2.1 copy-start.13
  193.6 0.7 copy-start.15
  202.2 1.0 copy-start.9
  202.2 1.1 copy-start.16
  203.3 3.7 %copy-start.7 = (bf16[384,512]{1,0:T(8,128)(2,1)S(1)}, bf16[384,512]{1,0:T(8,128)(2,1)}, u32[]{:S(2)}) copy-start(bf16[384,512]{1,0:T(8,128)(2,1)} %copy-done.6) | copy-start | bytes 1179652
  203.3 3.7 %copy-start.14 = (bf16[384,512]{1,0:T(8,128)(2,1)S(1)}, bf16[384,512]{1,0:T(8,128)(2,1)}, u32[]{:S(2)}) copy-start(bf16[384,512]{1,0:T(8,128)(2,1)} %copy-done.13) | copy-start | bytes 1179652
  212.2 51.7 %all-to-all-start.2 = ((bf16[64,6,1792]{2,1,0:T(8,128)(2,1)}), bf16[64,6,1792]{2,1,0:T(8,128)(2,1)S(1)}, u32[]{:S(2)}, u32[]{:S(2)}) async-start(bf16[64,6,1792]{2,1,0:T(8,128)(2,1)} %reshape.103), calls=%async_computation.2 | async-start | bytes 3670016 | tf_op jit(solution)/shard_map/all_to_all | solution.py:160
  267.5 40.6 %copy-start.1 = (bf16[128,7168]{1,0:T(8,128)(2,1)S(1)}, bf16[128,7168]{1,0:T(8,128)(2,1)}, u32[]{:S(2)}) copy-start(bf16[128,7168]{1,0:T(8,128)(2,1)} %param.9) | copy-start | bytes 5505028
Sparse Core Ops, SparseCore 0:
  11.0 111.4 all-gather.1
  202.4 102.3 reduce-scatter.1
where the time goes:
time: 316 us; the launch traced here: 315 us
  waiting for transfers between devices  186 us (59%)
  starting transfers between devices  45.9 us (15%)
  local copies, waits for them, and re-layouts  25.8 us (8%)
  matrix products  22 us (7%)
  other arithmetic  20.9 us (7%)
  between operations  14.5 us (5%)
    all_to_all x1, waiting for transfers between devices, body(): lax.all_to_all(expert_dx.reshape(devices_ep, capacity, quarter), 'ep', sp...  44.4 us
    all_to_all x1, waiting for transfers between devices, body(): lax.all_to_all(d_send, 'ep', split_axis=0, concat_axis=0, tiled=True)  41.8 us
    all_to_all x1, waiting for transfers between devices, body(): lax.all_to_all(x_send, 'ep', split_axis=0, concat_axis=0, tiled=True)  39.8 us
    reduce_scatter x1, waiting for transfers between devices, body(): lax.psum_scatter(jnp.concatenate([gate_term, up_term, down_term], axis=1)...  34.1 us
    ppermute x12, waiting for transfers between devices, from_partner(): return lax.ppermute(value, axis, pairs)  25.6 us
    ppermute x12, starting transfers between devices, from_partner(): return lax.ppermute(value, axis, pairs)  18.6 us
    all_to_all x1, starting transfers between devices, body(): lax.all_to_all(x_send, 'ep', split_axis=0, concat_axis=0, tiled=True)  13.3 us
    all_to_all x1, starting transfers between devices, body(): lax.all_to_all(expert_dx.reshape(devices_ep, capacity, quarter), 'ep', sp...  7.28 us
  transfers between devices with their start and end apart: 17, of which 12 were waited for; matrix products, arithmetic and copies ran while one was open for 14% of the time, Pallas kernels for 0%

commit v1 on v0

v1 whole, which is shorter than its diff:
```python
import functools

import jax
import jax.numpy as jnp
from jax import lax
from jax.experimental import pallas as pl
from jax.experimental.pallas import tpu as pltpu
from jax.sharding import PartitionSpec as P

D = 7168
GROUP = 4
CAP = 6
PLANE = 8
NT = (((1,), (1,)), ((), ()))
NN = (((1,), (0,)), ((), ()))
MESH = pl.DeviceIdType.MESH
BF = jnp.bfloat16
F32 = jnp.float32


class Copies:
    def __init__(self, send, recv):
        self.send, self.recv, self.used, self.open = send, recv, 0, []

    def slots(self, count):
        first = self.used
        self.used += count
        return first

    def make(self, src, dst, slot, device):
        return pltpu.make_async_remote_copy(
            src_ref=src,
            dst_ref=dst,
            send_sem=self.send.at[slot],
            recv_sem=self.recv.at[slot],
            device_id=device,
            device_id_type=MESH,
        )

    def start(self, src, dst, slot, device):
        copy = self.make(src, dst, slot, device)
        copy.start()
        self.open.append(copy)

    def arrived(self, dst, slot, device):
        self.make(dst, dst, slot, device).wait_recv()

    def drain(self):
        for copy in self.open:
            copy.wait_send()


def halves(width):
    return [(0, width // 2), (width // 2, width // 2)]


def pieces(width):
    unit = width // 7
    return [(0, 2 * unit), (2 * unit, 2 * unit), (4 * unit, 2 * unit), (6 * unit, unit)]


def semaphores(planes, plane):
    count = 4 * (plane - 1) + 4 * (planes - 1) + 4 * planes + 3 + 4 + 4 + 12 + 3
    return count + 4 + 4 * (planes - 1) + 4 * (plane - 1)


def kernel(
    planes, plane, cap,
    sel_ref, sel_t_ref, scale_ref, perm_ref, perm_t_ref,
    tok_hbm, grad_hbm, wg_hbm, wu_hbm, wd_hbm,
    out_ref, gout_ref,
    raw, send1, r1, r1p, xs, wv, gu_send, gu_recv, gu_keep, gu_send2, gu_recv2,
    bk_send, bk_recv, bk_keep, bk_send2, bk_recv2, gu_own, hid, dgu, dt,
    gterm, grecv, dx_send, dx_recv, dx_own, dxs, rz, rzp, ret,
    local_sem, send_sem, recv_sem,
):
    quarter = xs.shape[2]
    block = planes * cap
    rows = plane * block
    part = rows // 4
    units = wv.shape[1] // 2
    r = lax.axis_index("dp")
    ep = lax.axis_index("ep")
    z = ep // plane
    u = lax.rem(ep, plane)
    c = lax.rem(u, 2)
    bx = lax.rem(u // 2, 2)
    y_tok = r + 1 - 2 * lax.rem(r, 2)
    y_wt = 3 - r
    copies = Copies(send_sem, recv_sem)

    def in_plane(k):
        if k == 0:
            return u
        out = u
        for bit in range(3):
            if k >> bit & 1:
                out = out + (1 << bit) * (1 - 2 * lax.rem(u // (1 << bit), 2))
        return out

    def at_u(k):
        return (r, z * plane + in_plane(k))

    def z_to(k):
        return lax.rem(z + k, planes)

    def z_from(k):
        return lax.rem(z + planes - k, planes)

    def at_z(k):
        return (r, z_to(k) * plane + u)

    def from_z(k):
        return (r, z_from(k) * plane + u)

    def blk(index, size=None):
        size = block if size is None else size
        return pl.ds(pl.multiple_of(index * size, size), size)

    z_order = [1, planes - 1]
    for k in range(2, planes):
        if k not in z_order:
            z_order.append(k)
            if planes - k not in z_order:
                z_order.append(planes - k)
    z_order = list(dict.fromkeys(k for k in z_order if k % planes))
    u_order = [k for k in (4, 5, 2, 3, 6, 7, 1) if k < plane]
    token_y, weight_y = (y_tok, ep), (y_wt, ep)

    loads = [
        pltpu.make_async_copy(tok_hbm, raw.at[0], local_sem.at[0]),
        pltpu.make_async_copy(grad_hbm, raw.at[1], local_sem.at[1]),
    ]
    for w, ref in enumerate((wg_hbm, wu_hbm, wd_hbm)):
        loads.append(pltpu.make_async_copy(ref, wv.at[w, pl.ds(0, units)], local_sem.at[2 + w]))
    for load in loads:
        load.start()

    barrier = pltpu.get_barrier_semaphore()
    partners = [at_u(k) for k in u_order] + [at_z(k) for k in z_order] + [token_y, weight_y]
    for device in partners:
        pl.semaphore_signal(barrier, inc=1, device_id=device, device_id_type=MESH)
    pl.semaphore_wait(barrier, len(partners))

    w_slot = copies.slots(3)
    for w, ref in enumerate((wg_hbm, wu_hbm, wd_hbm)):
        copies.start(ref, wv.at[w, pl.ds(units, units)], w_slot + w, weight_y)

    chunks = halves(quarter)
    st1 = copies.slots(4 * (plane - 1))
    st2 = copies.slots(4 * (planes - 1))
    fwd = copies.slots(4 * planes)

    def gather(a, j):
        lo, width = chunks[j]
        for q in range(GROUP):
            got = lax.dot_general(
                sel_ref[...], raw[a, :, pl.ds(q * quarter + lo, width)], NN, preferred_element_type=F32
            )
            if a:
                got = got * scale_ref[...]
            got = got.astype(BF)
            for h in range(plane // GROUP):
                send1[a, h * GROUP + q, :, pl.ds(lo, width)] = got[h * block : (h + 1) * block]
        cols = pl.ds(lo, width)
        for k in u_order:
            copies.start(
                send1.at[a, in_plane(k), :, cols],
                r1.at[a, blk(u), cols],
                st1 + (2 * a + j) * (plane - 1) + k - 1,
                at_u(k),
            )
        r1[a, blk(u), cols] = send1[a, u, :, cols]

    def plane_stage(a, j):
        lo, width = chunks[j]
        cols = pl.ds(lo, width)
        for k in u_order:
            copies.arrived(
                r1.at[a, blk(in_plane(k)), cols], st1 + (2 * a + j) * (plane - 1) + k - 1, at_u(k)
            )
        r1p[a, :, cols] = lax.dot_general(
            perm_ref[...], r1[a, :, cols], NN, preferred_element_type=F32
        ).astype(BF)
        for k in z_order:
            copies.start(
                r1p.at[a, blk(z_to(k)), cols],
                xs.at[a, blk(z), cols],
                st2 + (2 * a + j) * (planes - 1) + k - 1,
                at_z(k),
            )
        xs[a, blk(z), cols] = r1p[a, blk(z), cols]

    def other(index):
        return pl.ds(pl.multiple_of(rows + index * block, block), block)

    def forward(a, j, which):
        lo, width = chunks[j]
        cols = pl.ds(lo, width)
        for k in which:
            zs = z_from(k)
            if k:
                copies.arrived(
                    xs.at[a, blk(zs), cols], st2 + (2 * a + j) * (planes - 1) + k - 1, from_z(k)
                )
            copies.start(
                xs.at[a, blk(zs), cols], xs.at[a, other(zs), cols], fwd + (2 * a + j) * planes + k, token_y
            )

    def forwarded(a):
        for j, (lo, width) in enumerate(chunks):
            for k in [0] + z_order:
                copies.arrived(
                    xs.at[a, other(z_from(k)), pl.ds(lo, width)], fwd + (2 * a + j) * planes + k, token_y
                )

    loads[0].wait()
    gather(0, 0)
    gather(0, 1)
    loads[1].wait()
    gather(1, 0)
    gather(1, 1)
    plane_stage(0, 0)
    plane_stage(0, 1)
    every = [0] + z_order
    first, last = every[: planes // 2], every[planes // 2 :]
    forward(0, 0, every)
    plane_stage(1, 0)
    forward(0, 1, every)
    plane_stage(1, 1)

    mine = c * 2 * part
    theirs = (1 - c) * 2 * part
    rs1 = copies.slots(4)
    rs2 = copies.slots(4)

    def rows_at(t, offset, size):
        return pl.ds(pl.multiple_of(t * rows + offset, part), size)

    def project(a, t, offset, kinds, dst):
        left = xs.at[a, rows_at(t, offset, 2 * part), :]

        def step(i, carry):
            w, b = kinds[0] + i // 2, lax.rem(i, 2)
            got = lax.dot_general(
                left[...],
                wv[w, pl.ds(pl.multiple_of(b * units, units), units), :],
                NT,
                preferred_element_type=F32,
            )
            dst[:, pl.ds(pl.multiple_of(i * units, units), units)] = got.astype(dst.dtype)
            return carry

        lax.fori_loop(0, 2 * len(kinds), step, 0)

    def to_core(a, t, kinds, send, recv, keep, slot):
        project(a, t, theirs, kinds, send.at[t])
        copies.start(send.at[t], recv.at[t], slot + t, at_u(1))
        project(a, t, mine, kinds, keep.at[t])

    def to_chip(t, recv, keep, send2, recv2, slot, slot2):
        copies.arrived(recv.at[t], slot + t, at_u(1))
        away = pl.ds(pl.multiple_of((1 - bx) * part, part), part)
        send2[t] = (keep[t, away, :] + recv[t, away, :].astype(F32)).astype(BF)
        copies.start(send2.at[t], recv2.at[t], slot2 + t, at_u(2))

    def summed(t, recv, keep, recv2, slot2):
        copies.arrived(recv2.at[t], slot2 + t, at_u(2))
        here = pl.ds(pl.multiple_of(bx * part, part), part)
        return keep[t, here, :] + recv[t, here, :].astype(F32) + recv2[t].astype(F32)

    def piece(t, core, side):
        return rows_at(t, core * 2 * part + side * part, part)

    def share(ref, t, slot):
        own = ref.at[piece(t, c, bx)]
        copies.start(own, own, slot, at_u(2))
        copies.start(own, own, slot + 1, at_u(1))

    def relay(ref, t, slot):
        theirs_too = ref.at[piece(t, c, 1 - bx)]
        copies.arrived(theirs_too, slot, at_u(2))
        copies.start(theirs_too, theirs_too, slot + 2, at_u(1))

    def gathered(ref, t, slot):
        copies.arrived(ref.at[piece(t, 1 - c, bx)], slot + 1, at_u(1))
        copies.arrived(ref.at[piece(t, 1 - c, 1 - bx)], slot + 2, at_u(1))

    ag = copies.slots(12)
    width_h = 2 * units

    def hidden(t):
        both = summed(t, gu_recv, gu_keep, gu_recv2, rs1 * 0 + rs2)
        gu_own[t] = both
        gate, up = both[:, :width_h], both[:, width_h:]
        hid[piece(t, c, bx)] = (gate * jax.nn.sigmoid(gate) * up).astype(BF)
        share(hid, t, ag + 3 * t)

    def gradients(t):
        back = summed(t, bk_recv, bk_keep, bk_recv2, rs2 + 2)
        gate, up = gu_own[t, :, :width_h], gu_own[t, :, width_h:]
        logistic = jax.nn.sigmoid(gate)
        own = piece(t, c, bx)
        dgu[own, :width_h] = (back * up * logistic * (1.0 + gate * (1.0 - logistic))).astype(BF)
        dgu[own, width_h:] = (back * (gate * logistic)).astype(BF)
        share(dgu, t, ag + 6 + 3 * t)

    for w in (0, 1):
        loads[2 + w].wait()
        copies.arrived(wv.at[w, pl.ds(units, units)], w_slot + w, weight_y)
    to_core(0, 0, (0, 1), gu_send, gu_recv, gu_keep, rs1)
    forward(1, 0, first)
    forwarded(0)
    to_core(0, 1, (0, 1), gu_send, gu_recv, gu_keep, rs1)
    to_chip(0, gu_recv, gu_keep, gu_send2, gu_recv2, rs1, rs2)
    to_chip(1, gu_recv, gu_keep, gu_send2, gu_recv2, rs1, rs2)
    forward(1, 0, last)
    hidden(0)
    hidden(1)
    forward(1, 1, first)
    relay(hid, 0, ag)
    relay(hid, 1, ag + 3)
    forward(1, 1, last)

    loads[4].wait()
    copies.arrived(wv.at[2, pl.ds(units, units)], w_slot + 2, weight_y)
    to_core(1, 0, (2,), bk_send, bk_recv, bk_keep, rs1 + 2)
    forwarded(1)
    to_core(1, 1, (2,), bk_send, bk_recv, bk_keep, rs1 + 2)
    to_chip(0, bk_recv, bk_keep, bk_send2, bk_recv2, rs1 + 2, rs2 + 2)
    to_chip(1, bk_recv, bk_keep, bk_send2, bk_recv2, rs1 + 2, rs2 + 2)

    gr = copies.slots(3)
    span = quarter // 7

    def grad_term(w, b, a, left, at):
        dt[...] = left[:, pl.ds(at + b * units, units)].T

        def step(i, carry):
            cols = pl.ds(pl.multiple_of(i * span, span), span)
            got = lax.dot_general(dt[...], xs[a, :, cols], NN, preferred_element_type=F32)
            gterm[b, w, :, cols] = got.astype(BF)
            return carry

        lax.fori_loop(0, 7, step, 0)
        if b:
            copies.start(gterm.at[1, w], grecv.at[w], gr + w, weight_y)

    gathered(hid, 0, ag)
    gathered(hid, 1, ag + 3)
    grad_term(2, 1, 1, hid, 0)
    gradients(0)
    gradients(1)
    relay(dgu, 0, ag + 6)
    relay(dgu, 1, ag + 9)
    gathered(dgu, 1, ag + 9)
    gathered(dgu, 0, ag + 6)

    parts = pieces(quarter)
    dxy = copies.slots(4)
    dxz = copies.slots(4 * (planes - 1))
    dxu = copies.slots(4 * (plane - 1))

    def dx_term(t, i):
        lo, width = parts[i]
        cols = pl.ds(lo, width)
        at = pl.ds(t * rows, rows)
        got = lax.dot_general(dgu[at, :width_h], wv[0, :, cols], NN, preferred_element_type=F32)
        return got + lax.dot_general(dgu[at, width_h:], wv[1, :, cols], NN, preferred_element_type=F32)

    def dx_out(i):
        lo, width = parts[i]
        cols = pl.ds(lo, width)
        dx_send[:, cols] = dx_term(1, i).astype(BF)
        copies.start(dx_send.at[:, cols], dx_recv.at[:, cols], dxy + i, token_y)

    def dx_here(i):
        lo, width = parts[i]
        dx_own[:, pl.ds(lo, width)] = dx_term(0, i)

    def dx_z(i):
        lo, width = parts[i]
        cols = pl.ds(lo, width)
        copies.arrived(dx_recv.at[:, cols], dxy + i, token_y)
        dxs[:, cols] = (dx_own[:, cols] + dx_recv[:, cols].astype(F32)).astype(BF)
        for k in z_order:
            copies.start(
                dxs.at[blk(z_to(k)), cols], rz.at[blk(z), cols], dxz + i * (planes - 1) + k - 1, at_z(k)
            )
        rz[blk(z), cols] = dxs[blk(z), cols]

    def dx_u(i):
        lo, width = parts[i]
        cols = pl.ds(lo, width)
        for k in z_order:
            copies.arrived(rz.at[blk(z_from(k)), cols], dxz + i * (planes - 1) + k - 1, from_z(k))
        rzp[:, cols] = lax.dot_general(
            perm_t_ref[...], rz[:, cols], NN, preferred_element_type=F32
        ).astype(BF)
        for k in u_order:
            copies.start(
                rzp.at[blk(in_plane(k)), cols], ret.at[u, :, cols], dxu + i * (plane - 1) + k - 1, at_u(k)
            )
        ret[u, :, cols] = rzp[blk(u), cols]

    def dx_back(i):
        lo, width = parts[i]
        cols = pl.ds(lo, width)
        for k in u_order:
            copies.arrived(ret.at[in_plane(k), :, cols], dxu + i * (plane - 1) + k - 1, at_u(k))
        for q in range(GROUP):
            total = None
            for h in range(plane // GROUP):
                got = lax.dot_general(
                    sel_t_ref[h], ret[h * GROUP + q, :, cols], NN, preferred_element_type=F32
                )
                total = got if total is None else total + got
            out_ref[:, pl.ds(q * quarter + lo, width)] = total.astype(BF)

    dx_out(0)
    grad_term(0, 1, 0, dgu, 0)
    dx_out(1)
    grad_term(1, 1, 0, dgu, width_h)
    dx_out(2)
    dx_out(3)
    for i in range(4):
        dx_here(i)
    dx_z(0)
    grad_term(0, 0, 0, dgu, 0)
    dx_z(1)
    dx_u(0)
    grad_term(1, 0, 0, dgu, width_h)
    dx_z(2)
    dx_u(1)
    grad_term(2, 0, 1, hid, 0)
    dx_z(3)
    dx_u(2)
    dx_u(3)
    for i in range(4):
        dx_back(i)

    for w in (2, 0, 1):
        copies.arrived(grecv.at[w], gr + w, weight_y)
        gout_ref[w] = (gterm[0, w].astype(F32) + grecv[w].astype(F32)).astype(BF)
    copies.drain()


def slot_choice(expert_ids, route_weight, order, capacity):
    experts = order.shape[0]
    ids = expert_ids.reshape(-1)
    count = ids.shape[0]
    same = (ids[:, None] == ids[None, :]) & (jnp.arange(count)[None, :] < jnp.arange(count)[:, None])
    ranks = jnp.sum(same.astype(jnp.int32), axis=1)
    expert_of_slot = jnp.repeat(order, capacity)
    rank_of_slot = jnp.tile(jnp.arange(capacity, dtype=jnp.int32), experts)
    match = (ids[None, :] == expert_of_slot[:, None]) & (ranks[None, :] == rank_of_slot[:, None])
    weight = jnp.sum(jnp.where(match, route_weight.reshape(-1)[None, :], 0.0), axis=1, keepdims=True)
    return match, weight


def body(planes, plane, capacity, tokens, out_grad, route_weight, expert_ids, w_gate, w_up, w_down):
    count, width = tokens.shape
    quarter = width // GROUP
    units = w_gate.shape[0]
    block = planes * capacity
    rows = plane * block
    part = rows // 4
    sides = plane // GROUP
    order = jnp.arange(planes * sides, dtype=jnp.int32).reshape(planes, sides).T.reshape(-1)
    match, weight = slot_choice(expert_ids, route_weight, order, capacity)
    sel = match.astype(BF)
    sel_t = sel.reshape(sides, block, count).transpose(0, 2, 1)
    at = jnp.arange(rows, dtype=jnp.int32)
    zi, ui, si = at // (plane * capacity), at // capacity % plane, at % capacity
    perm = (at[None, :] == (ui * block + zi * capacity + si)[:, None]).astype(BF)
    perm_t = (at[:, None] == (ui * block + zi * capacity + si)[None, :]).astype(BF)
    vmem = pl.BlockSpec(memory_space=pltpu.VMEM)
    hbm = pl.BlockSpec(memory_space=pl.ANY)
    sems = semaphores(planes, plane)
    in_grad, grads = pl.pallas_call(
        functools.partial(kernel, planes, plane, capacity),
        out_shape=(
            jax.ShapeDtypeStruct((count, width), BF),
            jax.ShapeDtypeStruct((3, units, quarter), BF),
        ),
        in_specs=[vmem] * 5 + [hbm] * 5,
        out_specs=(vmem, vmem),
        scratch_shapes=[
            pltpu.VMEM((2, count, width), BF),
            pltpu.VMEM((2, plane, block, quarter), BF),
            pltpu.VMEM((2, rows, quarter), BF),
            pltpu.VMEM((2, rows, quarter), BF),
            pltpu.VMEM((2, 2 * rows, quarter), BF),
            pltpu.VMEM((3, 2 * units, quarter), BF),
            pltpu.VMEM((2, 2 * part, 4 * units), BF),
            pltpu.VMEM((2, 2 * part, 4 * units), BF),
            pltpu.VMEM((2, 2 * part, 4 * units), F32),
            pltpu.VMEM((2, part, 4 * units), BF),
            pltpu.VMEM((2, part, 4 * units), BF),
            pltpu.VMEM((2, 2 * part, 2 * units), BF),
            pltpu.VMEM((2, 2 * part, 2 * units), BF),
            pltpu.VMEM((2, 2 * part, 2 * units), F32),
            pltpu.VMEM((2, part, 2 * units), BF),
            pltpu.VMEM((2, part, 2 * units), BF),
            pltpu.VMEM((2, part, 4 * units), F32),
            pltpu.VMEM((2 * rows, 2 * units), BF),
            pltpu.VMEM((2 * rows, 4 * units), BF),
            pltpu.VMEM((units, 2 * rows), BF),
            pltpu.VMEM((2, 3, units, quarter), BF),
            pltpu.VMEM((3, units, quarter), BF),
            pltpu.VMEM((rows, quarter), BF),
            pltpu.VMEM((rows, quarter), BF),
            pltpu.VMEM((rows, quarter), F32),
            pltpu.VMEM((rows, quarter), BF),
            pltpu.VMEM((rows, quarter), BF),
            pltpu.VMEM((rows, quarter), BF),
            pltpu.VMEM((plane, block, quarter), BF),
            pltpu.SemaphoreType.DMA((5,)),
            pltpu.SemaphoreType.DMA((sems,)),
            pltpu.SemaphoreType.DMA((sems,)),
        ],
        compiler_params=pltpu.CompilerParams(
            collective_id=0, has_side_effects=True, vmem_limit_bytes=63 * 1024 * 1024
        ),
        name="expert_backward",
    )(sel, sel_t, weight, perm, perm_t, tokens, out_grad, w_gate, w_up, w_down)
    return in_grad, grads[0], grads[1], grads[2]


def solution(mesh):
    tokens = P(("dp", "ep"), None)
    weights = P("dp", "ep")
    planes = mesh.shape["ep"] // PLANE
    return jax.shard_map(
        functools.partial(body, planes, PLANE, CAP),
        mesh=mesh,
        in_specs=(tokens, tokens, tokens, tokens, weights, weights, weights),
        out_specs=(tokens, weights, weights, weights),
        check_vma=False,
    )
```

time: 316 us -> 176 us (0.56)
  waiting for transfers between devices: 186 us -> 0 us
  Pallas kernels: 0 us -> 164 us
  starting transfers between devices: 45.9 us -> 0 us
  matrix products: 22 us -> 0 us
  local copies, waits for them, and re-layouts: 25.8 us -> 5.98 us
  other arithmetic: 20.9 us -> 5.47 us
  between operations: 14.5 us -> 0.68 us
    pallas_call x0 -> x1, Pallas kernels: none -> 164 us  [body(): pl.pallas_call(functools.partial(kernel, planes, plane, capacity), out_sh...]
    all_to_all x3 -> x0, waiting for transfers between devices: 126 us -> none  [the longest x1 44.4 us: body(): lax.all_to_all(expert_dx.reshape(devices_ep, capacity, quarter), 'ep', sp...]
    reduce_scatter x1 -> x0, waiting for transfers between devices: 34.1 us -> none  [body(): lax.psum_scatter(jnp.concatenate([gate_term, up_term, down_term], axis=1)...]
    all_to_all x3 -> x0, starting transfers between devices: 27.2 us -> none  [the longest x1 13.3 us: body(): lax.all_to_all(x_send, 'ep', split_axis=0, concat_axis=0, tiled=True)]
    ppermute x12 -> x0, waiting for transfers between devices: 25.6 us -> none  [from_partner(): return lax.ppermute(value, axis, pairs)]
    dot_general x8 -> x0, matrix products: 22 us -> none  [the longest x1 3.8 us: body(): lax.dot_general(x_used, gate_w, CONTRACT_LAST, preferred_element_type=jnp...]
    ppermute x12 -> x0, starting transfers between devices: 18.6 us -> none  [from_partner(): return lax.ppermute(value, axis, pairs)]
    concatenate x5 -> x0, other arithmetic: 12.7 us -> none  [the longest x1 5.73 us: body(): jnp.concatenate([gate_term, up_term, down_term], axis=1)]
  transfers between devices with their start and end apart: 17 -> 0, of which waited for: 12 -> 0; matrix products, arithmetic and copies ran while one was open for 14% -> 0% of each run, Pallas kernels for 0% -> 0%
where the time goes in v1:
time: 176 us
  Pallas kernels  164 us (93%)
  local copies, waits for them, and re-layouts  5.98 us (3%)
  other arithmetic  5.47 us (3%)
    pallas_call x1, Pallas kernels, body(): pl.pallas_call(functools.partial(kernel, planes, plane, capacity), out_sh...  164 us

profile of v1, /device:TPU:1, one launch (start us, length us, event | category | flops | bytes accessed | tf_op | source)
XLA Modules:
  0.0 176.2 jit_solution(10398620832889430589)
XLA Ops:
  0.6 0.9 convert_reduce_fusion
  1.5 0.1 reshape.137
  1.7 0.1 broadcast_in_dim.32
  1.7 0.1 broadcast_in_dim.33
  1.8 0.1 broadcast_in_dim.31
  1.9 0.1 eq.94
  2.0 0.1 eq.108
  2.1 0.1 eq.101
  2.2 0.9 select_reduce_fusion
  3.0 1.4 fusion.3.sel_ref
  4.4 0.7 copy.13.scale_ref
  5.1 1.4 and_convert_fusion.sel_t_ref
  6.5 0.9 fusion.1
  7.4 164.1 %expert_backward.1 = (bf16[128,7168]{1,0:T(8,128)(2,1)}, bf16[3,256,1792]{2,1,0:T(8,128)(2,1)}) custom-call(bf16[96,128]{1,0:T(8,128)(2,1)} %fusion.3.sel_ref, bf16[2,128,48]{2,1,0:T(8,128)(2,1)} %and_convert_fusion.sel_t_ref, f32[96,1]{1,0:T(8,128)} %copy.13.scale_ref, bf16[384,384]{1,0:T(8,128)(2,1)} %get-tuple-element.12.perm_ref, ...), custom_call_target="tpu_custom_call" | custom-call | tf_op jit(solution)/shard_map/expert_backward/pallas_call | solution.py:480
  171.5 0.0 copy-start
  171.5 3.5 %slice_bitcast_fusion = (bf16[256,1792]{1,0:T(8,128)(2,1)}, bf16[256,1792]{1,0:T(8,128)(2,1)}, bf16[256,1792]{1,0:T(8,128)(2,1)}) fusion(bf16[3,256,1792]{2,1,0:T(8,128)(2,1)} %get-tuple-element.7), kind=kLoop, calls=%fused_computation | loop fusion | bytes 5505024 | tf_op jit(solution)/shard_map/squeeze | solution.py:527
  175.0 0.0 copy-done
  175.0 1.2 copy.15
  (4 shorter events, 0.0 us)
Async XLA Ops:
  171.5 3.5 %copy-start = (bf16[128,7168]{1,0:T(8,128)(2,1)S(1)}, bf16[128,7168]{1,0:T(8,128)(2,1)}, u32[]{:S(2)}) copy-start(bf16[128,7168]{1,0:T(8,128)(2,1)} %get-tuple-element.17) | copy-start | bytes 5505028

commit v2 on v1

v2 whole, which is shorter than its diff:
```python
import functools

import jax
import jax.numpy as jnp
from jax import lax
from jax.experimental import pallas as pl
from jax.experimental.pallas import tpu as pltpu
from jax.sharding import PartitionSpec as P

D = 7168
GROUP = 4
CAP = 6
PLANE = 8
NT = (((1,), (1,)), ((), ()))
NN = (((1,), (0,)), ((), ()))
MESH = pl.DeviceIdType.MESH
BF = jnp.bfloat16
F32 = jnp.float32


def scope(stage):
    @functools.wraps(stage)
    def named(*args):
        tag = "_".join(str(a) for a in args if isinstance(a, int))
        with jax.named_scope(f"{stage.__name__}_{tag}"):
            return stage(*args)

    return named


class Copies:
    def __init__(self, send, recv):
        self.send, self.recv, self.sends, self.recvs, self.open = send, recv, 0, 0, []

    def sender(self, whole):
        self.open.append((whole, self.sends))
        self.sends += 1
        return self.sends - 1

    def slots(self, count):
        self.recvs += count
        return self.recvs - count

    def make(self, src, dst, sent, slot, device):
        return pltpu.make_async_remote_copy(
            src_ref=src,
            dst_ref=dst,
            send_sem=self.send.at[sent],
            recv_sem=self.recv.at[slot],
            device_id=device,
            device_id_type=MESH,
        )

    def start(self, src, dst, sent, slot, device):
        self.make(src, dst, sent, slot, device).start()

    def arrived(self, whole, slot, device):
        self.make(whole, whole, 0, slot, device).wait_recv()

    def drain(self, device):
        for whole, sent in self.open:
            self.make(whole, whole, sent, 0, device).wait_send()


def cut(width, sizes):
    unit, at, out = width // 14, 0, []
    for size in sizes:
        out.append((at, size * unit))
        at += size * unit
    return out


IN_CUTS = ((1, 2, 4, 4, 3), (4, 4, 4, 2))
OUT_CUT = (1, 3, 3, 3, 2, 1, 1)
GRAD_CUT = (4, 4, 4, 2)
SENDERS = 15


def receivers(planes):
    chunks = len(IN_CUTS[0]) + len(IN_CUTS[1])
    return chunks * (2 + planes // 2) + 3 * len(OUT_CUT) + 3 + 6 + 6 + 1 + 2 + 3


def slot_tables(planes, plane, cap, ids_ref, rw_ref, sel_ref, sel_t_ref, scale_ref, perm_ref, perm_t_ref):
    count = ids_ref.shape[1]
    block, rows, sides = planes * cap, perm_ref.shape[0], plane // GROUP
    by_col = jnp.broadcast_to(ids_ref[...].astype(F32), (count, count))
    by_row = by_col.T
    i = lax.broadcasted_iota(jnp.int32, (count, count), 0)
    j = lax.broadcasted_iota(jnp.int32, (count, count), 1)
    same = by_col == by_row
    rank_col = jnp.sum(jnp.where(same & (i < j), 1.0, 0.0), axis=0, keepdims=True)
    rank_row = jnp.sum(jnp.where(same & (j < i), 1.0, 0.0), axis=1, keepdims=True)

    def wanted(shape, axis, side_rows):
        at = lax.broadcasted_iota(jnp.int32, shape, axis)
        side, at = at // side_rows, lax.rem(at, side_rows)
        expert = at // cap * sides + side
        return expert.astype(F32), lax.rem(at, cap).astype(F32)

    expert, rank = wanted((sides * block, count), 0, block)
    match = (by_col[:1] == expert) & (rank_col == rank)
    sel_ref[...] = jnp.where(match, 1.0, 0.0).astype(BF)
    scale_ref[...] = jnp.sum(jnp.where(match, rw_ref[...], 0.0), axis=1, keepdims=True)
    expert, rank = wanted((count, block), 1, block)
    for side in range(sides):
        match = (by_row[:, :1] == expert + float(side)) & (rank_row == rank)
        sel_t_ref[side] = jnp.where(match, 1.0, 0.0).astype(BF)

    def source(shape, axis):
        at = lax.broadcasted_iota(jnp.int32, shape, axis)
        zi, rest = at // (plane * cap), lax.rem(at, plane * cap)
        return rest // cap * block + zi * cap + lax.rem(rest, cap)

    i = lax.broadcasted_iota(jnp.int32, (rows, rows), 0)
    j = lax.broadcasted_iota(jnp.int32, (rows, rows), 1)
    perm_ref[...] = jnp.where(source((rows, 1), 0) == j, 1.0, 0.0).astype(BF)
    perm_t_ref[...] = jnp.where(source((1, rows), 1) == i, 1.0, 0.0).astype(BF)


def kernel(
    planes, plane, cap,
    ids_ref, rw_ref, tok_hbm, grad_hbm, wg_hbm, wu_hbm, wd_hbm,
    out_ref, og_ref, ou_ref, od_ref,
    sel_ref, sel_t_ref, scale_ref, perm_ref, perm_t_ref, raw,
    send1, r1, r1p, xs, wgu, wdn, acc, core_out, core_in, chip_out, chip_in,
    hid, hid_t, dgu, dgu_t, gterm, gown, grecv, dx_send, dx_recv, dx_own, dxs, rz, rzp, ret,
    local_sem, send_sem, recv_sem,
):
    quarter = xs.shape[2]
    block = planes * cap
    rows = plane * block
    half = rows // 2
    units = hid.shape[1] // 2
    r = lax.axis_index("dp")
    ep = lax.axis_index("ep")
    z = ep // plane
    u = lax.rem(ep, plane)
    c = lax.rem(u, 2)
    copies = Copies(send_sem, recv_sem)

    def in_plane(k):
        out = u
        for bit in range(3):
            if k >> bit & 1:
                out = out + (1 << bit) * (1 - 2 * lax.rem(u // (1 << bit), 2))
        return out

    def at_u(k):
        return (r, z * plane + in_plane(k))

    def z_to(k):
        return lax.rem(z + k, planes)

    def z_from(k):
        return lax.rem(z + planes - k, planes)

    def at_z(k):
        return (r, z_to(k) * plane + u)

    def from_z(k):
        return (r, z_from(k) * plane + u)

    def blk(index):
        return pl.ds(pl.multiple_of(index * block, block), block)

    def other(index):
        return pl.ds(pl.multiple_of(rows + index * block, block), block)

    reach = [sorted({k, planes - k}) for k in range(1, planes // 2 + 1)]
    z_order = [k for group in reach for k in group]
    u_order = [k for k in (4, 5, 2, 3, 6, 7, 1) if k < plane]
    token_y, weight_y = (r + 1 - 2 * lax.rem(r, 2), ep), (3 - r, ep)

    own_w = (
        (wg_hbm, wgu.at[pl.ds(0, units)], wgu.at[pl.ds(2 * units, units)]),
        (wu_hbm, wgu.at[pl.ds(units, units)], wgu.at[pl.ds(3 * units, units)]),
        (wd_hbm, wdn.at[pl.ds(0, units)], wdn.at[pl.ds(units, units)]),
    )
    loads = [
        pltpu.make_async_copy(tok_hbm, raw.at[0], local_sem.at[0]),
        pltpu.make_async_copy(grad_hbm, raw.at[1], local_sem.at[1]),
    ]
    for w, (ref, here, _) in enumerate(own_w):
        loads.append(pltpu.make_async_copy(ref, here, local_sem.at[2 + w]))
    loads[0].start()

    barrier = pltpu.get_barrier_semaphore()
    partners = [at_u(k) for k in u_order] + [at_z(k) for k in z_order] + [token_y, weight_y]
    for device in partners:
        pl.semaphore_signal(barrier, inc=1, device_id=device, device_id_type=MESH)

    with jax.named_scope("tables"):
        slot_tables(
            planes, plane, cap, ids_ref, rw_ref, sel_ref, sel_t_ref, scale_ref, perm_ref, perm_t_ref
        )
    w_slot = copies.slots(3)
    w_sent = copies.sender(wgu.at[pl.ds(0, 3 * units)])

    @scope
    def weight_here(w):
        loads[2 + w].wait()

    @scope
    def weight(w):
        copies.arrived(own_w[w][2], w_slot + w, weight_y)

    chunks = [cut(quarter, sizes) for sizes in IN_CUTS]
    index = [[0, 1, 2, 3, 4], [5, 6, 7, 8]]
    total = len(IN_CUTS[0]) + len(IN_CUTS[1])
    st1, st2, fwd = copies.slots(total), copies.slots(total * len(reach)), copies.slots(total)
    st1_sent = [copies.sender(r1p.at[a, pl.ds(0, rows - block)]) for a in range(2)]
    st2_sent = [copies.sender(r1p.at[a, pl.ds(0, rows - rows // planes)]) for a in range(2)]
    fwd_sent = [copies.sender(xs.at[a, pl.ds(0, rows)]) for a in range(2)]

    @scope
    def gather(a, j):
        lo, width = chunks[a][j]
        cols = pl.ds(lo, width)
        for q in range(GROUP):
            got = lax.dot_general(
                sel_ref[...], raw[a, :, pl.ds(q * quarter + lo, width)], NN, preferred_element_type=F32
            )
            if a:
                got = got * scale_ref[...]
            got = got.astype(BF)
            for h in range(plane // GROUP):
                send1[a, h * GROUP + q, :, cols] = got[h * block : (h + 1) * block]
        r1[a, blk(u), cols] = send1[a, u, :, cols]

    @scope
    def to_plane(a, j):
        cols = pl.ds(*chunks[a][j])
        for k in u_order:
            copies.start(
                send1.at[a, in_plane(k), :, cols],
                r1.at[a, blk(u), cols],
                st1_sent[a],
                st1 + index[a][j],
                at_u(k),
            )

    @scope
    def plane_stage(a, j):
        cols = pl.ds(*chunks[a][j])
        copies.arrived(r1.at[a, pl.ds(0, rows - block), cols], st1 + index[a][j], at_u(1))
        r1p[a, :, cols] = lax.dot_general(
            perm_ref[...], r1[a, :, cols], NN, preferred_element_type=F32
        ).astype(BF)
        for g, group in enumerate(reach):
            for k in group:
                copies.start(
                    r1p.at[a, blk(z_to(k)), cols],
                    xs.at[a, blk(z), cols],
                    st2_sent[a],
                    st2 + index[a][j] * len(reach) + g,
                    at_z(k),
                )
        xs[a, blk(z), cols] = r1p[a, blk(z), cols]

    @scope
    def forward(a, j, g0, g1):
        cols = pl.ds(*chunks[a][j])
        for g in range(g0, min(g1, len(reach))):
            if g == 0:
                pass_on(a, j, 0)
            copies.arrived(
                xs.at[a, pl.ds(0, len(reach[g]) * block), cols],
                st2 + index[a][j] * len(reach) + g,
                at_z(1),
            )
            for k in reach[g]:
                pass_on(a, j, k)

    def pass_on(a, j, k):
        cols = pl.ds(*chunks[a][j])
        zs = z_from(k)
        copies.start(
            xs.at[a, blk(zs), cols], xs.at[a, other(zs), cols], fwd_sent[a], fwd + index[a][j], token_y
        )

    @scope
    def forwarded(a, j):
        cols = pl.ds(*chunks[a][j])
        copies.arrived(xs.at[a, pl.ds(rows, rows), cols], fwd + index[a][j], token_y)

    mine = lambda t: pl.ds(pl.multiple_of(t * rows + c * half, half), half)
    theirs = lambda t: pl.ds(pl.multiple_of(t * rows + (1 - c) * half, half), half)
    core = copies.slots(6)
    chip = copies.slots(6)
    share_h, share_d = copies.slots(1), copies.slots(2)
    core_sent, chip_sent = copies.sender(core_out), copies.sender(chip_out)
    h_sent, d_sent = copies.sender(hid.at[pl.ds(0, rows)]), copies.sender(dgu.at[pl.ds(0, rows)])
    span = 2 * units

    def project(left, weights, t, g, cols, add):
        at = pl.ds(t * rows, rows)

        def step(b, carry):
            got = lax.dot_general(
                left[at, cols],
                weights[pl.ds(pl.multiple_of(b * units, units), units), cols],
                NT,
                preferred_element_type=F32,
            )
            to = pl.ds(pl.multiple_of(g * span + b * units, units), units)
            acc[at, to] = acc[at, to] + got if add else got
            return carry

        lax.fori_loop(0, 2, step, 0)

    @scope
    def gate_up(t, b):
        project(xs.at[0], wgu.at[pl.ds(b * span, span)], t, b, pl.ds(0, quarter), False)

    @scope
    def back(t, j0, j1):
        lo = chunks[1][j0][0]
        width = sum(chunks[1][j1]) - lo
        project(xs.at[1], wdn, t, 2, pl.ds(lo, width), j0 > 0)

    @scope
    def to_core(t, g):
        cols = pl.ds(g * span, span)
        core_out[t, :, cols] = acc[theirs(t), cols].astype(BF)
        copies.start(core_out.at[t, :, cols], core_in.at[t, :, cols], core_sent, core + 3 * t + g, at_u(1))

    @scope
    def to_chip(t, g):
        cols = pl.ds(g * span, span)
        copies.arrived(core_in.at[t, :, cols], core + 3 * t + g, at_u(1))
        pair = acc[mine(t), cols] + core_in[t, :, cols].astype(F32)
        acc[mine(t), cols] = pair
        chip_out[t, :, cols] = pair.astype(BF)
        copies.start(chip_out.at[t, :, cols], chip_in.at[t, :, cols], chip_sent, chip + 3 * t + g, at_u(2))

    def summed(t, g):
        cols = pl.ds(g * span, span)
        copies.arrived(chip_in.at[t, :, cols], chip + 3 * t + g, at_u(2))
        return acc[mine(t), cols] + chip_in[t, :, cols].astype(F32)

    @scope
    def hidden(t, b):
        both = summed(t, b)
        acc[mine(t), pl.ds(b * span, span)] = both
        gate, up = both[:, :units], both[:, units:]
        at = hid.at[mine(t), pl.ds(b * units, units)]
        at[...] = (gate * jax.nn.sigmoid(gate) * up).astype(BF)
        copies.start(at, at, h_sent, share_h, at_u(1))

    @scope
    def gradients(t):
        both = summed(t, 2)
        for b in range(2):
            gate = acc[mine(t), pl.ds(b * span, units)]
            up = acc[mine(t), pl.ds(b * span + units, units)]
            grad = both[:, b * units : (b + 1) * units]
            logistic = jax.nn.sigmoid(gate)
            dgu[mine(t), pl.ds(b * span, units)] = (
                grad * up * logistic * (1.0 + gate * (1.0 - logistic))
            ).astype(BF)
            dgu[mine(t), pl.ds(b * span + units, units)] = (grad * (gate * logistic)).astype(BF)
        at = dgu.at[mine(t)]
        copies.start(at, at, d_sent, share_d + t, at_u(1))

    @scope
    def hidden_here():
        copies.arrived(hid.at[pl.ds(0, rows)], share_h, at_u(1))

    @scope
    def gradients_here(t):
        copies.arrived(dgu.at[theirs(t)], share_d + t, at_u(1))

    grad_cut = cut(quarter, GRAD_CUT)
    gr = copies.slots(3)
    gr_sent = copies.sender(gterm)

    @scope
    def flip_hidden():
        hid_t[...] = hid[...].T

    @scope
    def flip_gradients(b):
        dgu_t[pl.ds(b * span, span)] = dgu[:, pl.ds(b * span, span)].T

    @scope
    def down_out(i):
        cols = pl.ds(*grad_cut[i])
        gterm[2, :, cols] = lax.dot_general(
            hid_t[pl.ds(units, units)], xs[1, :, cols], NN, preferred_element_type=F32
        ).astype(BF)
        copies.start(gterm.at[2, :, cols], grecv.at[2, :, cols], gr_sent, gr + 2, weight_y)

    @scope
    def gate_up_out(i):
        cols = pl.ds(*grad_cut[i])
        for w in range(2):
            gterm[w, :, cols] = lax.dot_general(
                dgu_t[pl.ds(span + w * units, units)], xs[0, :, cols], NN, preferred_element_type=F32
            ).astype(BF)
            copies.start(gterm.at[w, :, cols], grecv.at[w, :, cols], gr_sent, gr + w, weight_y)

    @scope
    def term_here(w):
        left = hid_t.at[pl.ds(0, units)] if w == 2 else dgu_t.at[pl.ds(w * units, units)]
        for lo, width in grad_cut:
            cols = pl.ds(lo, width)
            gown[w, :, cols] = lax.dot_general(
                left[...], xs[w // 2, :, cols], NN, preferred_element_type=F32
            ).astype(BF)

    @scope
    def grad_out(w, ref):
        copies.arrived(grecv.at[w], gr + w, weight_y)
        ref[...] = (gown[w].astype(F32) + grecv[w].astype(F32)).astype(BF)

    parts = cut(quarter, OUT_CUT)
    dxy = copies.slots(len(parts))
    dxz, dxu = copies.slots(len(parts)), copies.slots(len(parts))
    dxy_sent = copies.sender(dx_send)
    dxz_sent = copies.sender(dxs.at[pl.ds(0, rows - rows // planes)])
    dxu_sent = copies.sender(dxs.at[pl.ds(0, rows - block)])

    def dx_term(t, cols):
        return lax.dot_general(
            dgu[pl.ds(t * rows, rows)], wgu[:, cols], NN, preferred_element_type=F32
        )

    @scope
    def dx_out(i):
        cols = pl.ds(*parts[i])
        dx_send[:, cols] = dx_term(1, cols).astype(BF)
        copies.start(dx_send.at[:, cols], dx_recv.at[:, cols], dxy_sent, dxy + i, token_y)

    @scope
    def dx_here(i):
        cols = pl.ds(*parts[i])
        dx_own[:, cols] = dx_term(0, cols)

    @scope
    def dx_z(i):
        cols = pl.ds(*parts[i])
        copies.arrived(dx_recv.at[:, cols], dxy + i, token_y)
        dxs[:, cols] = (dx_own[:, cols] + dx_recv[:, cols].astype(F32)).astype(BF)
        for k in reversed(z_order):
            copies.start(
                dxs.at[blk(z_to(k)), cols], rz.at[blk(z), cols], dxz_sent, dxz + i, at_z(k)
            )
        rz[blk(z), cols] = dxs[blk(z), cols]

    @scope
    def dx_u(i):
        cols = pl.ds(*parts[i])
        copies.arrived(rz.at[pl.ds(0, rows - rows // planes), cols], dxz + i, at_z(1))
        rzp[:, cols] = lax.dot_general(
            perm_t_ref[...], rz[:, cols], NN, preferred_element_type=F32
        ).astype(BF)
        for k in u_order:
            copies.start(
                rzp.at[blk(in_plane(k)), cols], ret.at[u, :, cols], dxu_sent, dxu + i, at_u(k)
            )
        ret[u, :, cols] = rzp[blk(u), cols]

    @scope
    def dx_back(i):
        lo, width = parts[i]
        cols = pl.ds(lo, width)
        copies.arrived(rz.at[pl.ds(0, rows - block), cols], dxu + i, at_u(1))
        for q in range(GROUP):
            total = None
            for h in range(plane // GROUP):
                got = lax.dot_general(
                    sel_t_ref[h], ret[h * GROUP + q, :, cols], NN, preferred_element_type=F32
                )
                total = got if total is None else total + got
            out_ref[:, pl.ds(q * quarter + lo, width)] = total.astype(BF)

    loads[0].wait()
    for load in loads[1:]:
        load.start()
    gather(0, 0)
    gather(0, 1)
    with jax.named_scope("barrier"):
        pl.semaphore_wait(barrier, len(partners))
    to_plane(0, 0)
    for w, (ref, _, there) in enumerate(own_w):
        copies.start(ref, there, w_sent, w_slot + w, weight_y)
    to_plane(0, 1)
    for j in range(2, 5):
        gather(0, j)
        to_plane(0, j)
    loads[1].wait()
    for j in range(4):
        gather(1, j)
        to_plane(1, j)
    plane_stage(0, 0)
    plane_stage(0, 1)
    forward(0, 0, 0, 4)
    plane_stage(0, 2)
    forward(0, 1, 0, 4)
    plane_stage(0, 3)
    forward(0, 2, 0, 4)
    plane_stage(0, 4)
    forward(0, 3, 0, 4)
    plane_stage(1, 0)
    forward(0, 4, 0, 4)
    plane_stage(1, 1)
    weight_here(0)
    weight_here(1)
    gate_up(0, 0)
    to_core(0, 0)
    forward(1, 0, 0, 1)
    for j in range(5):
        forwarded(0, j)
    gate_up(1, 0)
    to_core(1, 0)
    to_chip(0, 0)
    forward(1, 0, 1, 2)
    weight(0)
    weight(1)
    gate_up(0, 1)
    to_core(0, 1)
    to_chip(1, 0)
    gate_up(1, 1)
    to_core(1, 1)
    forward(1, 0, 2, 4)
    to_chip(0, 1)
    plane_stage(1, 2)
    to_chip(1, 1)
    plane_stage(1, 3)
    forward(1, 1, 0, 1)
    hidden(0, 0)
    forward(1, 1, 1, 4)
    hidden(1, 0)
    forward(1, 2, 0, 2)
    hidden(0, 1)
    forward(1, 2, 2, 3)
    hidden(1, 1)
    forward(1, 2, 3, 4)
    hidden_here()
    flip_hidden()
    forwarded(1, 0)
    down_out(0)
    forward(1, 3, 0, 1)
    forwarded(1, 1)
    down_out(1)
    weight_here(2)
    weight(2)
    forward(1, 3, 1, 2)
    back(0, 0, 2)
    forward(1, 3, 2, 3)
    back(1, 0, 1)
    forward(1, 3, 3, 4)
    back(0, 3, 3)
    to_core(0, 2)
    forwarded(1, 2)
    back(1, 2, 2)
    to_chip(0, 2)
    forwarded(1, 3)
    back(1, 3, 3)
    to_core(1, 2)
    down_out(2)
    to_chip(1, 2)
    gradients(0)
    down_out(3)
    gradients(1)
    gradients_here(0)
    gradients_here(1)
    dx_out(0)
    flip_gradients(1)
    gate_up_out(0)
    dx_out(1)
    gate_up_out(1)
    dx_out(2)
    dx_here(0)
    dx_z(0)
    dx_out(3)
    gate_up_out(2)
    dx_out(4)
    gate_up_out(3)
    dx_out(5)
    dx_out(6)
    dx_here(1)
    dx_here(2)
    dx_z(1)
    dx_u(0)
    for i in range(3, 7):
        dx_here(i)
    flip_gradients(0)
    dx_z(2)
    dx_u(1)
    dx_back(0)
    term_here(2)
    dx_z(3)
    dx_u(2)
    dx_back(1)
    dx_z(4)
    term_here(0)
    dx_z(5)
    dx_u(3)
    dx_back(2)
    dx_z(6)
    term_here(1)
    dx_u(4)
    grad_out(2, od_ref)
    dx_u(5)
    dx_back(3)
    dx_u(6)
    dx_back(4)
    dx_back(5)
    dx_back(6)
    grad_out(0, og_ref)
    grad_out(1, ou_ref)
    with jax.named_scope("drain"):
        copies.drain(token_y)
    assert (copies.sends, copies.recvs) == (SENDERS, receivers(planes))


def store(*refs):
    sems = refs[-1]
    moves = [pltpu.make_async_copy(refs[i], refs[4 + i], sems.at[i]) for i in range(4)]
    for move in moves:
        move.start()
    for move in moves:
        move.wait()


def body(planes, plane, capacity, tokens, out_grad, route_weight, expert_ids, w_gate, w_up, w_down):
    count, width = tokens.shape
    quarter = width // GROUP
    units = w_gate.shape[0]
    block = planes * capacity
    rows = plane * block
    half = rows // 2
    sides = plane // GROUP
    vmem = pl.BlockSpec(memory_space=pltpu.VMEM)
    hbm = pl.BlockSpec(memory_space=pl.ANY)
    results = pl.pallas_call(
        functools.partial(kernel, planes, plane, capacity),
        out_shape=(
            pltpu.VMEM((count, width), BF),
            pltpu.VMEM((units, quarter), BF),
            pltpu.VMEM((units, quarter), BF),
            pltpu.VMEM((units, quarter), BF),
        ),
        in_specs=[vmem] * 2 + [hbm] * 5,
        out_specs=(vmem,) * 4,
        scratch_shapes=[
            pltpu.VMEM((sides * block, count), BF),
            pltpu.VMEM((sides, count, block), BF),
            pltpu.VMEM((sides * block, 1), F32),
            pltpu.VMEM((rows, rows), BF),
            pltpu.VMEM((rows, rows), BF),
            pltpu.VMEM((2, count, width), BF),
            pltpu.VMEM((2, plane, block, quarter), BF),
            pltpu.VMEM((2, rows, quarter), BF),
            pltpu.VMEM((2, rows, quarter), BF),
            pltpu.VMEM((2, 2 * rows, quarter), BF),
            pltpu.VMEM((4 * units, quarter), BF),
            pltpu.VMEM((2 * units, quarter), BF),
            pltpu.VMEM((2 * rows, 6 * units), F32),
            pltpu.VMEM((2, half, 6 * units), BF),
            pltpu.VMEM((2, half, 6 * units), BF),
            pltpu.VMEM((2, half, 6 * units), BF),
            pltpu.VMEM((2, half, 6 * units), BF),
            pltpu.VMEM((2 * rows, 2 * units), BF),
            pltpu.VMEM((2 * units, 2 * rows), BF),
            pltpu.VMEM((2 * rows, 4 * units), BF),
            pltpu.VMEM((4 * units, 2 * rows), BF),
            pltpu.VMEM((3, units, quarter), BF),
            pltpu.VMEM((3, units, quarter), BF),
            pltpu.VMEM((3, units, quarter), BF),
            pltpu.VMEM((rows, quarter), BF),
            pltpu.VMEM((rows, quarter), BF),
            pltpu.VMEM((rows, quarter), F32),
            pltpu.VMEM((rows, quarter), BF),
            pltpu.VMEM((rows, quarter), BF),
            pltpu.VMEM((rows, quarter), BF),
            pltpu.VMEM((plane, block, quarter), BF),
            pltpu.SemaphoreType.DMA((5,)),
            pltpu.SemaphoreType.DMA((SENDERS,)),
            pltpu.SemaphoreType.DMA((receivers(planes),)),
        ],
        compiler_params=pltpu.CompilerParams(
            collective_id=0, has_side_effects=True, vmem_limit_bytes=58 * 1024 * 1024
        ),
        name="expert_backward",
    )(
        expert_ids.reshape(1, count), route_weight.reshape(1, count),
        tokens, out_grad, w_gate, w_up, w_down,
    )
    return pl.pallas_call(
        store,
        out_shape=tuple(jax.ShapeDtypeStruct(a.shape, a.dtype) for a in results),
        in_specs=[vmem] * 4,
        out_specs=(hbm,) * 4,
        scratch_shapes=[pltpu.SemaphoreType.DMA((4,))],
        compiler_params=pltpu.CompilerParams(vmem_limit_bytes=1024 * 1024),
        name="store",
    )(*(pltpu.with_memory_space_constraint(a, pltpu.VMEM) for a in results))


def solution(mesh):
    tokens = P(("dp", "ep"), None)
    weights = P("dp", "ep")
    planes = mesh.shape["ep"] // PLANE
    return jax.shard_map(
        functools.partial(body, planes, PLANE, CAP),
        mesh=mesh,
        in_specs=(tokens, tokens, tokens, tokens, weights, weights, weights),
        out_specs=(tokens, weights, weights, weights),
        check_vma=False,
    )
```

time: 176 us -> 143 us (0.81)
  Pallas kernels: 164 us -> 142 us
  local copies, waits for them, and re-layouts: 5.98 us -> 0 us
  other arithmetic: 5.47 us -> 0 us
    pallas_call x1, Pallas kernels: 164 us -> 139 us  [body(): pl.pallas_call(functools.partial(kernel, planes, plane, capacity), out_sh...]
    convert_element_type x3 -> x0, other arithmetic: 3.67 us -> none  [the longest x2 2.74 us: body(): sel = match.astype(BF)]
    squeeze x1 -> x0, local copies, waits for them, and re-layouts: 3.45 us -> none  [body(): return (in_grad, grads[0], grads[1], grads[2])]
    pallas_call x0 -> x1, Pallas kernels: none -> 2.17 us  [body(): pl.pallas_call(store, out_shape=tuple((jax.ShapeDtypeStruct(a.shape, a.dt...]
    reduce_sum x2 -> x0, other arithmetic: 1.77 us -> none  [the longest x1 0.9 us: slot_choice(): ranks = jnp.sum(same.astype(jnp.int32), axis=1)]
where the time goes in v2:
time: 143 us; the launch traced here: 142 us
  Pallas kernels  142 us (99%)
    pallas_call x1, Pallas kernels, body(): pl.pallas_call(functools.partial(kernel, planes, plane, capacity), out_sh...  139 us

profile of v2, /device:TPU:1, one launch (start us, length us, event | category | flops | bytes accessed | tf_op | source)
XLA Modules:
  0.0 142.4 jit_solution(17385666358715496940)
XLA Ops:
  0.6 139.5 %expert_backward.1 = (bf16[128,7168]{1,0:T(8,128)(2,1)S(1)}, bf16[256,1792]{1,0:T(8,128)(2,1)S(1)}, bf16[256,1792]{1,0:T(8,128)(2,1)S(1)}, bf16[256,1792]{1,0:T(8,128)(2,1)S(1)}) custom-call(s32[1,128]{1,0:T(1,128)} %bitcast.2, f32[1,128]{1,0:T(1,128)} %bitcast.3, bf16[128,7168]{1,0:T(8,128)(2,1)} %tok_hbm.1, bf16[128,7168]{1,0:T(8,128)(2,1)} %grad_hbm.1, ...), custom_call_target="tpu_custom_call" | custom-call | tf_op jit(solution)/shard_map/expert_backward/pallas_call | solution.py:638
  140.1 2.2 %store.1 = (bf16[128,7168]{1,0:T(8,128)(2,1)}, bf16[256,1792]{1,0:T(8,128)(2,1)}, bf16[256,1792]{1,0:T(8,128)(2,1)}, bf16[256,1792]{1,0:T(8,128)(2,1)}) custom-call(bf16[128,7168]{1,0:T(8,128)(2,1)S(1)} %get-tuple-element.8.refs_0_, bf16[256,1792]{1,0:T(8,128)(2,1)S(1)} %get-tuple-element.9.refs_1_, bf16[256,1792]{1,0:T(8,128)(2,1)S(1)} %get-tuple-element.10.refs_2_, ...), custom_call_target="tpu_custom_call" | custom-call | tf_op jit(solution)/shard_map/store/pallas_call | solution.py:692

commit v3 on v2

--- a/solution.py
+++ b/solution.py
@@ -70,15 +70,15 @@
     return out
 
 
-IN_CUTS = ((1, 2, 4, 4, 3), (4, 4, 4, 2))
-OUT_CUT = (1, 3, 3, 3, 2, 1, 1)
+IN_CUTS = ((2, 2, 3, 4, 3), (4, 4, 4, 2))
+OUT_CUT = (2, 2, 2, 2, 2, 2, 1, 1)
 GRAD_CUT = (4, 4, 4, 2)
 SENDERS = 15
 
 
 def receivers(planes):
     chunks = len(IN_CUTS[0]) + len(IN_CUTS[1])
-    return chunks * (2 + planes // 2) + 3 * len(OUT_CUT) + 3 + 6 + 6 + 1 + 2 + 3
+    return chunks * (2 + planes // 2) - planes // 2 + 1 + 3 * len(OUT_CUT) + 3 + 6 + 6 + 1 + 2 + 3
 
 
 def slot_tables(planes, plane, cap, ids_ref, rw_ref, sel_ref, sel_t_ref, scale_ref, perm_ref, perm_t_ref):
@@ -123,7 +123,7 @@
     ids_ref, rw_ref, tok_hbm, grad_hbm, wg_hbm, wu_hbm, wd_hbm,
     out_ref, og_ref, ou_ref, od_ref,
     sel_ref, sel_t_ref, scale_ref, perm_ref, perm_t_ref, raw,
-    send1, r1, r1p, xs, wgu, wdn, acc, core_out, core_in, chip_out, chip_in,
+    send1, ez, ez_in, er, r1, r1p, xs, wgu, wdn, acc, core_out, core_in, chip_out, chip_in,
     hid, hid_t, dgu, dgu_t, gterm, gown, grecv, dx_send, dx_recv, dx_own, dxs, rz, rzp, ret,
     local_sem, send_sem, recv_sem,
 ):
@@ -149,6 +149,9 @@
     def at_u(k):
         return (r, z * plane + in_plane(k))
 
+    def across(k):
+        return (r + 1 - 2 * lax.rem(r, 2), z * plane + in_plane(k))
+
     def z_to(k):
         return lax.rem(z + k, planes)
 
@@ -177,16 +180,28 @@
         (wu_hbm, wgu.at[pl.ds(units, units)], wgu.at[pl.ds(3 * units, units)]),
         (wd_hbm, wdn.at[pl.ds(0, units)], wdn.at[pl.ds(units, units)]),
     )
+    lead = quarter // 14 * sum(IN_CUTS[0][:2])
+    ahead = [
+        pltpu.make_async_copy(
+            tok_hbm.at[:, pl.ds(q * quarter + lo, width)],
+            raw.at[0, :, pl.ds(q * quarter + lo, width)],
+            local_sem.at[n],
+        )
+        for n, lo, width in ((5, 0, lead), (0, lead, quarter - lead))
+        for q in range(GROUP)
+    ]
     loads = [
-        pltpu.make_async_copy(tok_hbm, raw.at[0], local_sem.at[0]),
+        pltpu.make_async_copy(tok_hbm.at[:, pl.ds(0, GROUP * (quarter - lead))], raw.at[0, :, pl.ds(0, GROUP * (quarter - lead))], local_sem.at[0]),
         pltpu.make_async_copy(grad_hbm, raw.at[1], local_sem.at[1]),
     ]
     for w, (ref, here, _) in enumerate(own_w):
         loads.append(pltpu.make_async_copy(ref, here, local_sem.at[2 + w]))
-    loads[0].start()
+    for load in ahead:
+        load.start()
 
     barrier = pltpu.get_barrier_semaphore()
     partners = [at_u(k) for k in u_order] + [at_z(k) for k in z_order] + [token_y, weight_y]
+    partners += [across(k) for k in u_order]
     for device in partners:
         pl.semaphore_signal(barrier, inc=1, device_id=device, device_id_type=MESH)
 
@@ -208,7 +223,8 @@
     chunks = [cut(quarter, sizes) for sizes in IN_CUTS]
     index = [[0, 1, 2, 3, 4], [5, 6, 7, 8]]
     total = len(IN_CUTS[0]) + len(IN_CUTS[1])
-    st1, st2, fwd = copies.slots(total), copies.slots(total * len(reach)), copies.slots(total)
+    st1, fwd = copies.slots(total), copies.slots(total)
+    early, st2 = copies.slots(1), copies.slots((total - 1) * len(reach)) - len(reach)
     st1_sent = [copies.sender(r1p.at[a, pl.ds(0, rows - block)]) for a in range(2)]
     st2_sent = [copies.sender(r1p.at[a, pl.ds(0, rows - rows // planes)]) for a in range(2)]
     fwd_sent = [copies.sender(xs.at[a, pl.ds(0, rows)]) for a in range(2)]
@@ -225,15 +241,15 @@
                 got = got * scale_ref[...]
             got = got.astype(BF)
             for h in range(plane // GROUP):
-                send1[a, h * GROUP + q, :, cols] = got[h * block : (h + 1) * block]
-        r1[a, blk(u), cols] = send1[a, u, :, cols]
+                send1[a, pl.ds((h * GROUP + q) * block, block), cols] = got[h * block : (h + 1) * block]
 
     @scope
     def to_plane(a, j):
         cols = pl.ds(*chunks[a][j])
+        r1[a, blk(u), cols] = send1[a, blk(u), cols]
         for k in u_order:
             copies.start(
-                send1.at[a, in_plane(k), :, cols],
+                send1.at[a, blk(in_plane(k)), cols],
                 r1.at[a, blk(u), cols],
                 st1_sent[a],
                 st1 + index[a][j],
@@ -257,13 +273,50 @@
                     at_z(k),
                 )
         xs[a, blk(z), cols] = r1p[a, blk(z), cols]
+        pass_on(a, j, 0)
+
+    first = pl.ds(*chunks[0][0])
+
+    @scope
+    def early_z():
+        ez[...] = lax.dot_general(
+            perm_ref[...], send1[0, :, first], NN, preferred_element_type=F32
+        ).astype(BF)
+        for k in z_order:
+            copies.start(ez.at[blk(z_to(k))], ez_in.at[blk(z)], st2_sent[0], early, at_z(k))
+        ez_in[blk(z)] = ez[blk(z)]
+
+    @scope
+    def early_plane():
+        copies.arrived(ez_in.at[pl.ds(0, rows - rows // planes)], early, at_z(1))
+        r1p[0, :, first] = lax.dot_general(
+            perm_t_ref[...], ez_in[...], NN, preferred_element_type=F32
+        ).astype(BF)
+        for k in u_order:
+            copies.start(
+                r1p.at[0, blk(in_plane(k)), first], r1.at[0, blk(u), first], st1_sent[0], st1, at_u(k)
+            )
+        for k in [0] + u_order:
+            copies.start(
+                r1p.at[0, blk(in_plane(k)), first], er.at[blk(u)], fwd_sent[0], fwd, across(k)
+            )
+        r1[0, blk(u), first] = r1p[0, blk(u), first]
+
+    @scope
+    def early_here(t):
+        if t:
+            copies.arrived(er, fwd, token_y)
+        else:
+            copies.arrived(r1.at[0, pl.ds(0, rows - block), first], st1, at_u(1))
+        src = er[...] if t else r1[0, :, first]
+        xs[0, pl.ds(t * rows, rows), first] = lax.dot_general(
+            perm_ref[...], src, NN, preferred_element_type=F32
+        ).astype(BF)
 
     @scope
     def forward(a, j, g0, g1):
         cols = pl.ds(*chunks[a][j])
         for g in range(g0, min(g1, len(reach))):
-            if g == 0:
-                pass_on(a, j, 0)
             copies.arrived(
                 xs.at[a, pl.ds(0, len(reach[g]) * block), cols],
                 st2 + index[a][j] * len(reach) + g,
@@ -475,33 +528,44 @@
                 total = got if total is None else total + got
             out_ref[:, pl.ds(q * quarter + lo, width)] = total.astype(BF)
 
-    loads[0].wait()
+    pltpu.make_async_copy(
+        tok_hbm.at[:, pl.ds(0, GROUP * lead)], raw.at[0, :, pl.ds(0, GROUP * lead)], local_sem.at[5]
+    ).wait()
     for load in loads[1:]:
         load.start()
     gather(0, 0)
     gather(0, 1)
     with jax.named_scope("barrier"):
         pl.semaphore_wait(barrier, len(partners))
-    to_plane(0, 0)
+    to_plane(0, 1)
+    early_z()
     for w, (ref, _, there) in enumerate(own_w):
         copies.start(ref, there, w_sent, w_slot + w, weight_y)
-    to_plane(0, 1)
+    loads[0].wait()
     for j in range(2, 5):
         gather(0, j)
         to_plane(0, j)
     loads[1].wait()
-    for j in range(4):
-        gather(1, j)
-        to_plane(1, j)
-    plane_stage(0, 0)
+    gather(1, 0)
+    gather(1, 1)
     plane_stage(0, 1)
-    forward(0, 0, 0, 4)
+    early_plane()
     plane_stage(0, 2)
+    to_plane(1, 0)
+    to_plane(1, 1)
+    gather(1, 2)
+    to_plane(1, 2)
+    gather(1, 3)
+    to_plane(1, 3)
     forward(0, 1, 0, 4)
     plane_stage(0, 3)
-    forward(0, 2, 0, 4)
+    forward(0, 2, 0, 2)
+    early_here(0)
+    forward(0, 2, 2, 4)
     plane_stage(0, 4)
-    forward(0, 3, 0, 4)
+    forward(0, 3, 0, 1)
+    early_here(1)
+    forward(0, 3, 1, 4)
     plane_stage(1, 0)
     forward(0, 4, 0, 4)
     plane_stage(1, 1)
@@ -510,7 +574,7 @@
     gate_up(0, 0)
     to_core(0, 0)
     forward(1, 0, 0, 1)
-    for j in range(5):
+    for j in range(1, 5):
         forwarded(0, j)
     gate_up(1, 0)
     to_core(1, 0)
@@ -573,42 +637,49 @@
     gate_up_out(1)
     dx_out(2)
     dx_here(0)
-    dx_z(0)
     dx_out(3)
     gate_up_out(2)
+    dx_z(0)
     dx_out(4)
     gate_up_out(3)
     dx_out(5)
+    dx_here(1)
+    dx_z(1)
     dx_out(6)
-    dx_here(1)
+    dx_out(7)
     dx_here(2)
-    dx_z(1)
+    dx_here(3)
+    dx_z(2)
     dx_u(0)
-    for i in range(3, 7):
-        dx_here(i)
+    dx_here(4)
+    dx_here(5)
+    dx_z(3)
+    dx_u(1)
+    dx_here(6)
+    dx_here(7)
     flip_gradients(0)
-    dx_z(2)
-    dx_u(1)
+    dx_z(4)
+    dx_u(2)
     dx_back(0)
     term_here(2)
-    dx_z(3)
-    dx_u(2)
-    dx_back(1)
-    dx_z(4)
-    term_here(0)
     dx_z(5)
     dx_u(3)
+    dx_back(1)
+    term_here(0)
+    dx_z(6)
+    dx_u(4)
     dx_back(2)
-    dx_z(6)
+    dx_z(7)
     term_here(1)
-    dx_u(4)
-    grad_out(2, od_ref)
     dx_u(5)
     dx_back(3)
     dx_u(6)
     dx_back(4)
+    dx_u(7)
+    grad_out(2, od_ref)
     dx_back(5)
     dx_back(6)
+    dx_back(7)
     grad_out(0, og_ref)
     grad_out(1, ou_ref)
     with jax.named_scope("drain"):
@@ -652,7 +723,10 @@
             pltpu.VMEM((rows, rows), BF),
             pltpu.VMEM((rows, rows), BF),
             pltpu.VMEM((2, count, width), BF),
-            pltpu.VMEM((2, plane, block, quarter), BF),
+            pltpu.VMEM((2, rows, quarter), BF),
+            pltpu.VMEM((rows, quarter // 14 * IN_CUTS[0][0]), BF),
+            pltpu.VMEM((rows, quarter // 14 * IN_CUTS[0][0]), BF),
+            pltpu.VMEM((rows, quarter // 14 * IN_CUTS[0][0]), BF),
             pltpu.VMEM((2, rows, quarter), BF),
             pltpu.VMEM((2, rows, quarter), BF),
             pltpu.VMEM((2, 2 * rows, quarter), BF),
@@ -677,7 +751,7 @@
             pltpu.VMEM((rows, quarter), BF),
             pltpu.VMEM((rows, quarter), BF),
             pltpu.VMEM((plane, block, quarter), BF),
-            pltpu.SemaphoreType.DMA((5,)),
+            pltpu.SemaphoreType.DMA((6,)),
             pltpu.SemaphoreType.DMA((SENDERS,)),
             pltpu.SemaphoreType.DMA((receivers(planes),)),
         ],

time: 143 us -> 138 us (0.965)
  Pallas kernels: 142 us -> 137 us
    pallas_call x1, Pallas kernels: 139 us -> 135 us  [body(): pl.pallas_call(functools.partial(kernel, planes, plane, capacity), out_sh...]
where the time goes in v3:
time: 138 us
  Pallas kernels  137 us (99%)
    pallas_call x1, Pallas kernels, body(): pl.pallas_call(functools.partial(kernel, planes, plane, capacity), out_sh...  135 us

profile of v3, /device:TPU:1, one launch (start us, length us, event | category | flops | bytes accessed | tf_op | source)
XLA Modules:
  0.0 137.7 jit_solution(2936139451706969030)
XLA Ops:
  0.6 134.8 %expert_backward.1 = (bf16[128,7168]{1,0:T(8,128)(2,1)S(1)}, bf16[256,1792]{1,0:T(8,128)(2,1)S(1)}, bf16[256,1792]{1,0:T(8,128)(2,1)S(1)}, bf16[256,1792]{1,0:T(8,128)(2,1)S(1)}) custom-call(s32[1,128]{1,0:T(1,128)} %bitcast.2, f32[1,128]{1,0:T(1,128)} %bitcast.3, bf16[128,7168]{1,0:T(8,128)(2,1)} %tok_hbm.1, bf16[128,7168]{1,0:T(8,128)(2,1)} %grad_hbm.1, ...), custom_call_target="tpu_custom_call" | custom-call | tf_op jit(solution)/shard_map/expert_backward/pallas_call | solution.py:709
  135.4 2.2 %store.1 = (bf16[128,7168]{1,0:T(8,128)(2,1)}, bf16[256,1792]{1,0:T(8,128)(2,1)}, bf16[256,1792]{1,0:T(8,128)(2,1)}, bf16[256,1792]{1,0:T(8,128)(2,1)}) custom-call(bf16[128,7168]{1,0:T(8,128)(2,1)S(1)} %get-tuple-element.8.refs_0_, bf16[256,1792]{1,0:T(8,128)(2,1)S(1)} %get-tuple-element.9.refs_1_, bf16[256,1792]{1,0:T(8,128)(2,1)S(1)} %get-tuple-element.10.refs_2_, ...), custom_call_target="tpu_custom_call" | custom-call | tf_op jit(solution)/shard_map/store/pallas_call | solution.py:766

commit v4 on v3

--- a/solution.py
+++ b/solution.py
@@ -537,10 +537,10 @@
     gather(0, 1)
     with jax.named_scope("barrier"):
         pl.semaphore_wait(barrier, len(partners))
+    for w, (ref, _, there) in enumerate(own_w):
+        copies.start(ref, there, w_sent, w_slot + w, weight_y)
     to_plane(0, 1)
     early_z()
-    for w, (ref, _, there) in enumerate(own_w):
-        copies.start(ref, there, w_sent, w_slot + w, weight_y)
     loads[0].wait()
     for j in range(2, 5):
         gather(0, j)
@@ -574,11 +574,11 @@
     gate_up(0, 0)
     to_core(0, 0)
     forward(1, 0, 0, 1)
+    to_chip(0, 0)
     for j in range(1, 5):
         forwarded(0, j)
     gate_up(1, 0)
     to_core(1, 0)
-    to_chip(0, 0)
     forward(1, 0, 1, 2)
     weight(0)
     weight(1)
@@ -600,11 +600,11 @@
     hidden(0, 1)
     forward(1, 2, 2, 3)
     hidden(1, 1)
-    forward(1, 2, 3, 4)
     hidden_here()
     flip_hidden()
     forwarded(1, 0)
     down_out(0)
+    forward(1, 2, 3, 4)
     forward(1, 3, 0, 1)
     forwarded(1, 1)
     down_out(1)

time: 138 us -> 138 us (level)
  no operation moved by 1% of the time
where the time goes in v4:
time: 138 us; the launch traced here: 137 us
  Pallas kernels  137 us (99%)
    pallas_call x1, Pallas kernels, body(): pl.pallas_call(functools.partial(kernel, planes, plane, capacity), out_sh...  135 us

profile of v4, /device:TPU:1, one launch (start us, length us, event | category | flops | bytes accessed | tf_op | source)
XLA Modules:
  0.0 137.5 jit_solution(9428409942186776452)
XLA Ops:
  0.6 134.5 %expert_backward.1 = (bf16[128,7168]{1,0:T(8,128)(2,1)S(1)}, bf16[256,1792]{1,0:T(8,128)(2,1)S(1)}, bf16[256,1792]{1,0:T(8,128)(2,1)S(1)}, bf16[256,1792]{1,0:T(8,128)(2,1)S(1)}) custom-call(s32[1,128]{1,0:T(1,128)} %bitcast.2, f32[1,128]{1,0:T(1,128)} %bitcast.3, bf16[128,7168]{1,0:T(8,128)(2,1)} %tok_hbm.1, bf16[128,7168]{1,0:T(8,128)(2,1)} %grad_hbm.1, ...), custom_call_target="tpu_custom_call" | custom-call | tf_op jit(solution)/shard_map/expert_backward/pallas_call | solution.py:709
  135.1 2.2 %store.1 = (bf16[128,7168]{1,0:T(8,128)(2,1)}, bf16[256,1792]{1,0:T(8,128)(2,1)}, bf16[256,1792]{1,0:T(8,128)(2,1)}, bf16[256,1792]{1,0:T(8,128)(2,1)}) custom-call(bf16[128,7168]{1,0:T(8,128)(2,1)S(1)} %get-tuple-element.8.refs_0_, bf16[256,1792]{1,0:T(8,128)(2,1)S(1)} %get-tuple-element.9.refs_1_, bf16[256,1792]{1,0:T(8,128)(2,1)S(1)} %get-tuple-element.10.refs_2_, ...), custom_call_target="tpu_custom_call" | custom-call | tf_op jit(solution)/shard_map/store/pallas_call | solution.py:766

commit v5 on v4

--- a/solution.py
+++ b/solution.py
@@ -658,19 +658,19 @@
     dx_here(6)
     dx_here(7)
     flip_gradients(0)
+    term_here(0)
     dx_z(4)
     dx_u(2)
     dx_back(0)
     term_here(2)
+    term_here(1)
     dx_z(5)
     dx_u(3)
     dx_back(1)
-    term_here(0)
     dx_z(6)
     dx_u(4)
     dx_back(2)
     dx_z(7)
-    term_here(1)
     dx_u(5)
     dx_back(3)
     dx_u(6)

time: 138 us -> 138 us (level)
  no operation moved by 1% of the time
where the time goes in v5:
time: 138 us; the launch traced here: 137 us
  Pallas kernels  137 us (99%)
    pallas_call x1, Pallas kernels, body(): pl.pallas_call(functools.partial(kernel, planes, plane, capacity), out_sh...  135 us

profile of v5, /device:TPU:1, one launch (start us, length us, event | category | flops | bytes accessed | tf_op | source)
XLA Modules:
  0.0 137.5 jit_solution(14915343820007411032)
XLA Ops:
  0.6 134.5 %expert_backward.1 = (bf16[128,7168]{1,0:T(8,128)(2,1)S(1)}, bf16[256,1792]{1,0:T(8,128)(2,1)S(1)}, bf16[256,1792]{1,0:T(8,128)(2,1)S(1)}, bf16[256,1792]{1,0:T(8,128)(2,1)S(1)}) custom-call(s32[1,128]{1,0:T(1,128)} %bitcast.2, f32[1,128]{1,0:T(1,128)} %bitcast.3, bf16[128,7168]{1,0:T(8,128)(2,1)} %tok_hbm.1, bf16[128,7168]{1,0:T(8,128)(2,1)} %grad_hbm.1, ...), custom_call_target="tpu_custom_call" | custom-call | tf_op jit(solution)/shard_map/expert_backward/pallas_call | solution.py:709
  135.1 2.2 %store.1 = (bf16[128,7168]{1,0:T(8,128)(2,1)}, bf16[256,1792]{1,0:T(8,128)(2,1)}, bf16[256,1792]{1,0:T(8,128)(2,1)}, bf16[256,1792]{1,0:T(8,128)(2,1)}) custom-call(bf16[128,7168]{1,0:T(8,128)(2,1)S(1)} %get-tuple-element.8.refs_0_, bf16[256,1792]{1,0:T(8,128)(2,1)S(1)} %get-tuple-element.9.refs_1_, bf16[256,1792]{1,0:T(8,128)(2,1)S(1)} %get-tuple-element.10.refs_2_, ...), custom_call_target="tpu_custom_call" | custom-call | tf_op jit(solution)/shard_map/store/pallas_call | solution.py:766
